TPU v7x, 256 devices: a whole 4x4x8 slice. The times are simulated.
256 devices in a mesh: band: 128 (over x_lo, z, y, core), spin: 2 (over x_hi).
Axes of the slice: x: 4 (x_hi: 2, x_lo: 2; x = x_hi * 2 + x_lo), y: 4, z: 8, core: 2. Of those that a mesh axis runs over, the one named last changes fastest.
Arguments:
- coefficients: bfloat16 [2, 2, 256, 524288], P('spin', None, 'band'), may hold values from -1 to 1
- occupation: int32 [2, 256], P('spin', 'band'), may hold values from 0 to 1000
- miller: int32 [3, 524288], P(None, ('band', 'spin')), may hold values from -8 to 8
- density: float32 [2, 256, 128, 128], P('spin', 'band'), may hold values from 0.25 to 2
- local_factor: float32 [2, 256, 128, 128], P(None, None, 'band'), may hold values from -1.2 to 1.2
Outputs:
- stress: float32 [6], replicated
- kinetic_density: float32 [524288], P(('band', 'spin'))
- gradient_square: float32 [2, 256, 128, 128], P('spin', 'band')
All inputs are finite; a program needn't handle non-finite values.
Results may differ from a plain program's by a relative error of at most 0.0003.
Values sent between devices are 32-bit elements; how exact they have to be, the bound alone decides.
A program may use at most 64 MiB of HBM per device.

v0:
```python
import jax
import jax.numpy as jnp
from jax import lax
from jax.sharding import Mesh
from jax.sharding import PartitionSpec as P

NPW = 524288
NX = 128
NY = 128
NZ = 256
BAND_SPIN = ("band_0", "band_1", "band_2", "band_3", "spin")
BAND = ("band_0", "band_1", "band_2", "band_3")


occupation_unit = 1000.0
kpoint = (0.25, 0.125, 0.375)
spacing = 0.25


def sent_together(arrays, axis, split_dim, concat_dim, along):
    both = jnp.concatenate(arrays, axis=along)
    result, at, gathered = (
        lax.all_to_all(both, axis, split_axis=split_dim, concat_axis=concat_dim, tiled=True),
        0,
        [],
    )
    for a in arrays:
        gathered.append(lax.slice_in_dim(result, at, at + a.shape[along], axis=along))
        at += a.shape[along]
    return tuple(gathered)


def sent_to_all(shard, axis):
    length = lax.axis_size(axis)
    return lax.all_to_all(
        jnp.broadcast_to(shard[None], (length, *shard.shape)), axis, 0, 0, tiled=True
    )


def over_copies(shard, axis):
    return sent_to_all(shard, axis).sum(axis=0)


def packed_total(arrays, axis):
    flat, at, gathered = (jnp.concatenate([a.reshape(-1) for a in arrays]), 0, [])
    subtotal = over_copies(flat, axis)
    for a in arrays:
        gathered.append(subtotal[at : at + a.size].reshape(a.shape))
        at += a.size
    return tuple(gathered)


def by_axis(shard, axes):
    for axis in axes:
        shard = lax.psum(shard, axis)
    return shard


def derivative_table(length):
    row_index = jnp.arange(length, dtype=jnp.int32)[:, None]
    col_index = jnp.arange(length, dtype=jnp.int32)[None, :]
    wrapped = jnp.mod(row_index - col_index, length)
    angles = jnp.pi / length * wrapped.astype(jnp.float32)
    on_diagonal = wrapped == 0
    sines = jnp.where(on_diagonal, 1.0, jnp.sin(angles))
    parity = 1.0 - 2.0 * jnp.mod(wrapped, 2).astype(jnp.float32)
    return jnp.where(on_diagonal, 0.0, 0.5 * parity * jnp.cos(angles) / sines)


def fourier_tables(length):
    positions = jnp.arange(length, dtype=jnp.int32)
    phases = jnp.mod(positions[:, None] * positions[None, :], length).astype(jnp.float32) * (
        2.0 * jnp.pi / length
    )
    return (jnp.cos(phases), jnp.sin(phases))


def frequencies(length):
    positions = jnp.arange(length, dtype=jnp.int32)
    signed = jnp.where(positions >= length // 2, positions - length, positions)
    return 2.0 * jnp.pi / length * signed.astype(jnp.float32)


def six_sums(weighting, first_axis, second_axis, third_axis):
    return jnp.stack(
        [
            jnp.sum(weighting * first_axis * first_axis),
            jnp.sum(weighting * second_axis * second_axis),
            jnp.sum(weighting * third_axis * third_axis),
            jnp.sum(weighting * second_axis * third_axis),
            jnp.sum(weighting * first_axis * third_axis),
            jnp.sum(weighting * first_axis * second_axis),
        ]
    )


def xc_terms(dens_part, grad_x, grad_y, grad_z, cell_count):
    square = grad_x * grad_x + grad_y * grad_y + grad_z * grad_z
    kernel = dens_part ** (-1.0 / 3.0) / (1.0 + square / (4.0 * dens_part * dens_part + 1.0))
    return (square, -six_sums(kernel, grad_x, grad_y, grad_z) / cell_count)


def shards(coefficients, occupation, miller, density, local_factor):
    highest = lax.Precision.HIGHEST
    weights = occupation.astype(jnp.float32) / occupation_unit
    piece = coefficients.astype(jnp.float32)
    squares = piece[0, 0] * piece[0, 0] + piece[0, 1] * piece[0, 1]
    kinetic_weight = lax.psum_scatter(
        jnp.dot(weights[0], squares, precision=highest), BAND_SPIN, scatter_dimension=0, tiled=True
    )
    kvec = jnp.array(kpoint, jnp.float32)
    gvec = spacing * (miller.astype(jnp.float32) + kvec[:, None])
    kinetic_density = 0.5 * (gvec[0] ** 2 + gvec[1] ** 2 + gvec[2] ** 2) * kinetic_weight
    kinetic_stress = -six_sums(kinetic_weight, gvec[0], gvec[1], gvec[2]) / NPW
    band_devices = lax.axis_size(BAND)
    cell_count = density.shape[1] * band_devices * density.shape[2] * density.shape[3]
    deriv_x = derivative_table(NX)
    deriv_y = derivative_table(NY)
    deriv_z = derivative_table(NZ)
    cosine_x, sine_x = fourier_tables(NX)
    cosine_y, sine_y = fourier_tables(NY)
    cosine_z, sine_z = fourier_tables(NZ)
    grad_x = jnp.einsum("ik,szky->sziy", deriv_x, density, precision=highest)
    grad_y = jnp.einsum("ik,szxk->szxi", deriv_y, density, precision=highest)
    along_real = jnp.einsum("mj,szxj->szxm", cosine_y, density, precision=highest)
    along_imag = -jnp.einsum("mj,szxj->szxm", sine_y, density, precision=highest)
    plane_real = jnp.einsum("mj,szjy->szmy", cosine_x, along_real, precision=highest) + jnp.einsum(
        "mj,szjy->szmy", sine_x, along_imag, precision=highest
    )
    plane_imag = jnp.einsum("mj,szjy->szmy", cosine_x, along_imag, precision=highest) - jnp.einsum(
        "mj,szjy->szmy", sine_x, along_real, precision=highest
    )
    dens_col, real_col, imag_col = sent_together((density, plane_real, plane_imag), BAND, 2, 1, 0)
    gradz_col = jnp.einsum("ik,skxy->sixy", deriv_z, dens_col, precision=highest)
    grad_z = lax.all_to_all(gradz_col, BAND, split_axis=1, concat_axis=2, tiled=True)
    gradient_square, xc_stress = xc_terms(density, grad_x, grad_y, grad_z, cell_count)
    spec_real = (
        jnp.einsum("mj,jxy->mxy", cosine_z, real_col[0], precision=highest)
        + jnp.einsum("mj,jxy->mxy", sine_z, imag_col[0], precision=highest)
    ) / cell_count
    spec_imag = (
        jnp.einsum("mj,jxy->mxy", cosine_z, imag_col[0], precision=highest)
        - jnp.einsum("mj,jxy->mxy", sine_z, real_col[0], precision=highest)
    ) / cell_count
    total_real, total_imag = packed_total((spec_real, spec_imag), "spin")
    local_rows = real_col.shape[2]
    first_column = lax.axis_index(BAND) * local_rows
    freq_z = frequencies(NZ)[:, None, None]
    freq_x = lax.dynamic_slice_in_dim(frequencies(NX), first_column, local_rows, 0)[None, :, None]
    freq_y = frequencies(NY)[None, None, :]
    length_sq = freq_x * freq_x + freq_y * freq_y + freq_z * freq_z
    positive = length_sq > 0
    inverse = jnp.where(positive, 1.0 / jnp.where(positive, length_sq, 1.0), 0.0)
    hartree_weight = 4.0 * jnp.pi * (total_real * total_real + total_imag * total_imag) * inverse
    diagonal = jnp.array([1.0, 1.0, 1.0, 0.0, 0.0, 0.0], jnp.float32)
    hartree_stress = 2.0 * six_sums(
        hartree_weight * inverse, freq_x, freq_y, freq_z
    ) - diagonal * jnp.sum(hartree_weight)
    local_weight = 2.0 * (total_real * local_factor[0] + total_imag * local_factor[1])
    local_stress = six_sums(local_weight, freq_x, freq_y, freq_z)
    spin_share = 1.0 / lax.axis_size("spin")
    partial_stress = kinetic_stress + spin_share * (hartree_stress + local_stress) + xc_stress
    stress = by_axis(partial_stress, BAND_SPIN)
    return (stress, kinetic_density, gradient_square)


def solution(mesh):
    finer = Mesh(
        mesh.devices.reshape(2, 8, 4, 2, mesh.shape["spin"]),
        ("band_0", "band_1", "band_2", "band_3", "spin"),
    )
    return jax.shard_map(
        shards,
        mesh=finer,
        in_specs=(
            P("spin", None, BAND, None),
            P("spin", BAND),
            P(None, BAND_SPIN),
            P("spin", BAND, None, None),
            P(None, None, BAND, None),
        ),
        out_specs=(P(), P(BAND_SPIN), P("spin", BAND, None, None)),
        check_vma=False,
    )
```

profile of v0, /device:TPU:1, one launch (start us, length us, event | category | flops | bytes accessed | tf_op | source)
XLA Modules:
  0.0 368.5 jit_solution(17116945878228844177)
XLA Ops:
  7.2 1.4 fusion.10
  8.6 1.4 convolution_bitcast_fusion.2
  10.0 1.0 copy.33
  11.0 0.5 fusion.89
  11.5 0.5 fusion.91
  12.0 0.5 fusion.8
  12.6 0.5 fusion.9
  13.1 0.9 copy.34
  14.0 14.9 %all-to-all-start = ((f32[3,2,128,128]{3,1,0,2:T(2,128)}), f32[3,2,128,128]{3,1,0,2:T(2,128)S(1)}, u32[]{:S(2)}, u32[]{:S(2)}) async-start(f32[3,2,128,128]{3,1,0,2:T(2,128)} %copy.34), calls=%async_computation | async-start | bytes 786432 | tf_op jit(solution)/shard_map/all_to_all | solution.py:23
  28.9 0.2 all-reduce.3.cloned.1.call-start
  29.1 4.7 %convert_element_type.100 = f32[1,2,2,524288]{3,2,1,0:T(2,128)S(1)} convert(bf16[1,2,2,524288]{3,2,1,0:T(2,128)(2,1)} %param.7) | non-fusion elementwise | flops 2097152 | bytes 12582912 | tf_op jit(solution)/shard_map/convert_element_type | solution.py:106
  33.9 0.0 copy-start.1
  33.9 0.0 copy-start.3
  33.9 17.0 %fusion.2 = f32[1,524288]{1,0:T(1,128)} fusion(f32[1,2,2,524288]{3,2,1,0:T(2,128)S(1)} %convert_element_type.100, s32[1,2]{1,0:T(1,128)S(1)} %copy-done.5), kind=kOutput, calls=%fused_computation.4 | convolution fusion | flops 15728644 | bytes 10485768 | tf_op jit(solution)/shard_map/dot_general | solution.py:109
  51.0 0.0 all-reduce.3.cloned.1.call-update
  51.1 0.6 convolution_bitcast_fusion.1
  51.7 0.6 dynamic_slice.3
  53.9 0.1 add_multiply_fusion
  54.0 0.1 fusion.193
  54.2 1.6 fusion.68
  55.8 1.6 fusion.66
  57.3 1.6 fusion.7
  58.9 1.6 fusion.5
  60.5 1.6 convolution_bitcast_fusion
  62.0 0.0 copy-start.4
  62.1 0.8 copy.38
  62.8 12.4 %all-to-all-start.2 = ((f32[1,256,1,128]{3,2,0,1:T(1,128)}), f32[1,256,1,128]{3,2,0,1:T(1,128)S(1)}, u32[]{:S(2)}, u32[]{:S(2)}) async-start(f32[1,256,1,128]{3,2,0,1:T(1,128)} %copy.38), calls=%async_computation.2 | async-start | bytes 262144 | tf_op jit(solution)/shard_map/all_to_all | solution.py:135
  75.3 12.4 %all-to-all-done.2 = f32[1,256,1,128]{3,2,0,1:T(1,128)S(1)} async-done(((f32[1,256,1,128]{3,2,0,1:T(1,128)}), f32[1,256,1,128]{3,2,0,1:T(1,128)S(1)}, u32[]{:S(2)}, u32[]{:S(2)}) %all-to-all-start.2) | async-done | bytes 131104 | tf_op jit(solution)/shard_map/all_to_all | solution.py:135
  87.7 1.1 broadcast_in_dim.16
  88.7 3.8 %all-to-all-start.1 = ((f32[2,1,65536]{2,1,0:T(1,128)}), f32[2,1,65536]{2,1,0:T(1,128)S(1)}, u32[]{:S(2)}, u32[]{:S(2)}) async-start(f32[2,1,65536]{2,1,0:T(1,128)} %broadcast_in_dim.16), calls=%async_computation.1 | async-start | bytes 1048576 | tf_op jit(solution)/shard_map/all_to_all | solution.py:35
  92.6 1.3 fusion.40
  93.9 0.8 fusion.45
  94.7 3.9 %stack.111 = f32[6]{0:T(128)S(1)} concatenate(f32[1]{0:T(128)} %bitcast.60, f32[1]{0:T(128)} %bitcast.62, f32[1]{0:T(128)} %bitcast.64, f32[1]{0:T(128)} %bitcast.65, f32[1]{0:T(128)} %bitcast.66, f32[1]{0:T(128)} %bitcast.68), dimensions={0} | concatenate | bytes 48 | tf_op jit(solution)/shard_map/stack | solution.py:85
  98.5 3.1 all-to-all-done.1
  101.6 0.7 reduce_sum.240
  102.3 0.7 fusion.102
  103.0 1.4 multiply_reduce_fusion.2
  104.4 3.8 %stack.97 = f32[6]{0:T(128)S(1)} concatenate(f32[1]{0:T(128)} %bitcast.33, f32[1]{0:T(128)} %bitcast.34, f32[1]{0:T(128)} %bitcast.35, f32[1]{0:T(128)} %bitcast.36, f32[1]{0:T(128)} %bitcast.37, f32[1]{0:T(128)} %bitcast.38), dimensions={0} | concatenate | bytes 48 | tf_op jit(solution)/shard_map/stack | solution.py:85
  108.2 3.8 %stack.104 = f32[6]{0:T(128)S(1)} concatenate(f32[1]{0:T(128)} %bitcast.42, f32[1]{0:T(128)} %bitcast.43, f32[1]{0:T(128)} %bitcast.44, f32[1]{0:T(128)} %bitcast.45, f32[1]{0:T(128)} %bitcast.46, f32[1]{0:T(128)} %bitcast.47), dimensions={0} | concatenate | bytes 48 | tf_op jit(solution)/shard_map/stack | solution.py:85
  111.9 203.4 %all-reduce.3.cloned.1.call-done = f32[524288]{0:T(1024)} async-done(((f32[524288]{0:T(1024)}), f32[524288]{0:T(1024)}) %all-reduce.3.cloned.1.call-update) | async-done | bytes 2097168
  315.4 2.0 multiply_reduce_fusion.13
  317.3 3.7 %stack.90 = f32[6]{0:T(128)S(1)} concatenate(f32[1]{0:T(128)} %bitcast.5, f32[1]{0:T(128)} %bitcast.7, f32[1]{0:T(128)} %bitcast.9, f32[1]{0:T(128)} %bitcast.10, f32[1]{0:T(128)} %bitcast.11, f32[1]{0:T(128)} %bitcast.12), dimensions={0} | concatenate | bytes 48 | tf_op jit(solution)/shard_map/stack | solution.py:85
  321.0 0.7 multiply_add_fusion
  321.7 3.8 %psum.35 = f32[6]{0:T(128)S(1)} all-reduce(f32[6]{0:T(128)S(1)} %multiply_add_fusion), channel_id=1, replica_groups=mesh['band_0'=2,'band_1'=8,'band_2'=4,'band_3'=2,'spin'=2] {'band_0'}, use_global_device_ids=true, to_apply=%region_27.28 | all-reduce | flops 6 | bytes 48 | tf_op jit(solution)/shard_map/psum | solution.py:55
  325.5 14.7 %psum.36 = f32[6]{0:T(128)S(1)} all-reduce(f32[6]{0:T(128)S(1)} %psum.35), channel_id=1, replica_groups=mesh['band_0'=2,'band_1'=8,'band_2'=4,'band_3'=2,'spin'=2] {'band_1'}, use_global_device_ids=true, to_apply=%region_28.29 | all-reduce | flops 6 | bytes 48 | tf_op jit(solution)/shard_map/psum | solution.py:55
  340.1 8.2 %psum.37 = f32[6]{0:T(128)S(1)} all-reduce(f32[6]{0:T(128)S(1)} %psum.36), channel_id=1, replica_groups=mesh['band_0'=2,'band_1'=8,'band_2'=4,'band_3'=2,'spin'=2] {'band_2'}, use_global_device_ids=true, to_apply=%region_29.30 | all-reduce | flops 6 | bytes 48 | tf_op jit(solution)/shard_map/psum | solution.py:55
  348.3 7.6 %psum.38 = f32[6]{0:T(128)S(1)} all-reduce(f32[6]{0:T(128)S(1)} %psum.37), channel_id=1, replica_groups=mesh['band_0'=2,'band_1'=8,'band_2'=4,'band_3'=2,'spin'=2] {'band_3'}, use_global_device_ids=true, to_apply=%region_30.31 | all-reduce | flops 6 | bytes 48 | tf_op jit(solution)/shard_map/psum | solution.py:55
  355.9 5.8 %psum.39 = f32[6]{0:T(128)} all-reduce(f32[6]{0:T(128)S(1)} %psum.38), channel_id=1, replica_groups=mesh['band_0'=2,'band_1'=8,'band_2'=4,'band_3'=2,'spin'=2] {'spin'}, use_global_device_ids=true, to_apply=%region_31.32 | all-reduce | flops 6 | bytes 48 | tf_op jit(solution)/shard_map/psum | solution.py:55
  (18 shorter events, 0.1 us)
Async XLA Ops:
  14.0 40.0 %all-to-all-start = ((f32[3,2,128,128]{3,1,0,2:T(2,128)}), f32[3,2,128,128]{3,1,0,2:T(2,128)S(1)}, u32[]{:S(2)}, u32[]{:S(2)}) async-start(f32[3,2,128,128]{3,1,0,2:T(2,128)} %copy.34), calls=%async_computation | async-start | bytes 786432 | tf_op jit(solution)/shard_map/all_to_all | solution.py:23
  28.9 5.0 %copy-start.5 = (s32[1,2]{1,0:T(1,128)S(1)}, s32[1,2]{1,0:T(1,128)}, u32[]{:S(2)}) copy-start(s32[1,2]{1,0:T(1,128)} %param.8) | copy-start | bytes 28
  28.9 286.4 %all-reduce.3.cloned.1.call-start = ((), (), s32[]{:S(2)}) async-start(), calls=%async_computation.3 | async-start | bytes 4194304
  33.9 17.2 %copy-start.1 = (f32[1,2,128,128]{3,2,1,0:T(8,128)S(1)}, f32[1,2,128,128]{3,2,1,0:T(8,128)}, u32[]{:S(2)}) copy-start(f32[1,2,128,128]{3,2,1,0:T(8,128)} %param.10) | copy-start | bytes 393220
  33.9 19.4 %copy-start = (f32[2,256,1,128]{3,2,1,0:T(1,128)S(1)}, f32[2,256,1,128]{3,2,1,0:T(1,128)}, u32[]{:S(2)}) copy-start(f32[2,256,1,128]{3,2,1,0:T(1,128)} %param.11) | copy-start | bytes 786436
  33.9 20.0 %copy-start.2 = (s32[3,2048]{1,0:T(4,128)S(1)}, s32[3,2048]{1,0:T(4,128)}, u32[]{:S(2)}) copy-start(s32[3,2048]{1,0:T(4,128)} %param.9) | copy-start | bytes 73732
  33.9 20.0 %copy-start.3 = (f32[3]{0:T(128)S(1)}, f32[3]{0:T(128)}, u32[]{:S(2)}) copy-start(f32[3]{0:T(128)} %constant.152.clone) | copy-start | bytes 40
  62.0 259.0 %copy-start.4 = (f32[6]{0:T(128)S(1)}, f32[6]{0:T(128)}, u32[]{:S(2)}) copy-start(f32[6]{0:T(128)} %constant.153.clone) | copy-start | bytes 76
  62.8 24.9 %all-to-all-start.2 = ((f32[1,256,1,128]{3,2,0,1:T(1,128)}), f32[1,256,1,128]{3,2,0,1:T(1,128)S(1)}, u32[]{:S(2)}, u32[]{:S(2)}) async-start(f32[1,256,1,128]{3,2,0,1:T(1,128)} %copy.38), calls=%async_computation.2 | async-start | bytes 262144 | tf_op jit(solution)/shard_map/all_to_all | solution.py:135
  88.7 12.9 %all-to-all-start.1 = ((f32[2,1,65536]{2,1,0:T(1,128)}), f32[2,1,65536]{2,1,0:T(1,128)S(1)}, u32[]{:S(2)}, u32[]{:S(2)}) async-start(f32[2,1,65536]{2,1,0:T(1,128)} %broadcast_in_dim.16), calls=%async_computation.1 | async-start | bytes 1048576 | tf_op jit(solution)/shard_map/all_to_all | solution.py:35
Sparse Core Ops, SparseCore 0:
  51.1 264.1 all-reduce.2
where the time goes:
time: 369 us
  waiting for transfers between devices  219 us (59%)
  blocking collectives  40 us (11%)
  matrix products  31.6 us (9%)
  starting transfers between devices  31.3 us (8%)
  local copies, waits for them, and re-layouts  19.6 us (5%)
  between operations  16 us (4%)
  other arithmetic  11.1 us (3%)
    unnamed x2, waiting for transfers between devices  203 us
    psum x5, blocking collectives, by_axis(): shard = lax.psum(shard, axis)  40 us
    dot_general x1, matrix products, shards(): jnp.dot(weights[0], squares, precision=highest)  17 us
    another operation x4, local copies, waits for them, and re-layouts, six_sums(): jnp.stack([jnp.sum(weighting * first_axis * first_axis), jnp.sum(weightin...  15.1 us
    all_to_all x1, starting transfers between devices, sent_together(): lax.all_to_all(both, axis, split_axis=split_dim, concat_axis=concat_dim,...  14.9 us
    all_to_all x1, starting transfers between devices, shards(): lax.all_to_all(gradz_col, BAND, split_axis=1, concat_axis=2, tiled=True)  12.4 us
    all_to_all x1, waiting for transfers between devices, shards(): lax.all_to_all(gradz_col, BAND, split_axis=1, concat_axis=2, tiled=True)  12.4 us
  transfers between devices with their start and end apart: 4, of which 3 were waited for; matrix products, arithmetic and copies ran while one was open for 13% of the time, Pallas kernels for 0%

commit v1 on v0

--- a/solution.py
+++ b/solution.py
@@ -1,6 +1,8 @@
 import jax
 import jax.numpy as jnp
 from jax import lax
+from jax.experimental import pallas as pl
+from jax.experimental.pallas import tpu as pltpu
 from jax.sharding import Mesh
 from jax.sharding import PartitionSpec as P
 
@@ -48,12 +50,6 @@
         gathered.append(subtotal[at : at + a.size].reshape(a.shape))
         at += a.size
     return tuple(gathered)
-
-
-def by_axis(shard, axes):
-    for axis in axes:
-        shard = lax.psum(shard, axis)
-    return shard
 
 
 def derivative_table(length):
@@ -100,18 +96,204 @@
     return (square, -six_sums(kernel, grad_x, grad_y, grad_z) / cell_count)
 
 
+AXIS_X, AXIS_XLO, AXIS_Z, AXIS_Y, AXIS_C = "spin", "band_0", "band_1", "band_2", "band_3"
+MESH = pl.DeviceIdType.MESH
+
+
+def place():
+    x = lax.axis_index(AXIS_X) * 2 + lax.axis_index(AXIS_XLO)
+    return x, lax.axis_index(AXIS_Z), lax.axis_index(AXIS_Y), lax.axis_index(AXIS_C)
+
+
+def at_x(x):
+    return {AXIS_X: x // 2, AXIS_XLO: x % 2}
+
+
+def greet(groups):
+    barrier = pltpu.get_barrier_semaphore()
+    for peer in groups:
+        pl.semaphore_signal(barrier, inc=1, device_id=peer, device_id_type=MESH)
+    pl.semaphore_wait(barrier, len(groups))
+
+
+def kinetic_kernel(occ, coef, miller, density, tile, part, twin, qa, qb, ra, rb, a1, b1, ra2, rb2, ab, rz, tmp, ssem, rsem):
+    x, z, y, c = place()
+    other = 1 - c
+    x_peers = [lax.rem(x + d, 4) for d in (1, 2, 3)]
+    y_peers = [lax.rem(y + d, 4) for d in (1, 2, 3)]
+    z_peers = [lax.rem(z + d, 8) for d in range(1, 8)]
+    greet(
+        [{AXIS_C: other}]
+        + [at_x(p) for p in x_peers]
+        + [{AXIS_Y: p} for p in y_peers]
+        + [{AXIS_Z: p} for p in z_peers]
+    )
+    pending = []
+
+    def send(src, dst, k, peer):
+        copy = pltpu.make_async_remote_copy(
+            src_ref=src, dst_ref=dst, send_sem=ssem.at[k], recv_sem=rsem.at[k], device_id=peer, device_id_type=MESH
+        )
+        copy.start()
+        pending.append(copy)
+        return copy
+
+    w0 = jnp.full((64, 128), occ[0, 0].astype(jnp.float32)) / occupation_unit
+    w1 = jnp.full((64, 128), occ[0, 1].astype(jnp.float32)) / occupation_unit
+    twins = []
+    for q in range(4):
+
+        def squares(i, carry):
+            rows = pl.ds(pl.multiple_of(i * 128, 128), 128)
+            re = coef[0, rows, :].astype(jnp.float32)
+            im = coef[1, rows, :].astype(jnp.float32)
+            tmp[...] = re * re + im * im
+            both = w0 * tmp[pl.ds(0, 64, stride=2), :] + w1 * tmp[pl.ds(1, 64, stride=2), :]
+            part[i] = both.reshape(2, 32, 128)
+            return carry
+
+        lax.fori_loop(q * 16, q * 16 + 16, squares, 0)
+        twins.append(send(part.at[pl.ds(q * 16, 16), other], twin.at[pl.ds(q * 16, 16)], q, {AXIS_C: other}))
+    for q in range(4):
+        twins[q].wait_recv()
+
+        def add_twin(i, carry):
+            x_lo, zz, yy = i // 32, lax.rem(i // 4, 8), lax.rem(i, 4)
+            v = part[i, c] + twin[i]
+            for x_hi in range(2):
+                pos = x_hi * 2 + x_lo
+                qa[pos, yy * 8 + zz] = v[x_hi * 16 : x_hi * 16 + 8]
+                qb[yy, pos * 8 + zz] = v[x_hi * 16 + 8 : x_hi * 16 + 16]
+            return carry
+
+        lax.fori_loop(q * 16, q * 16 + 16, add_twin, 0)
+    first_a = [send(qa.at[p], ra.at[d], 4 + d, at_x(p)) for d, p in enumerate(x_peers)]
+    first_b = [send(qb.at[p], rb.at[d], 7 + d, {AXIS_Y: p}) for d, p in enumerate(y_peers)]
+    for copy in first_a:
+        copy.wait_recv()
+    for t in range(4):
+        sub = pl.ds(t * 8, 8)
+        a1[t] = (qa[x, sub] + ra[0, sub]) + (ra[1, sub] + ra[2, sub])
+    second_a = [send(a1.at[p], ra2.at[d], 10 + d, {AXIS_Y: p}) for d, p in enumerate(y_peers)]
+    for copy in first_b:
+        copy.wait_recv()
+    for t in range(4):
+        sub = pl.ds(t * 8, 8)
+        b1[t] = (qb[y, sub] + rb[0, sub]) + (rb[1, sub] + rb[2, sub])
+    second_b = [send(b1.at[p], rb2.at[d], 13 + d, at_x(p)) for d, p in enumerate(x_peers)]
+    for copy in second_a:
+        copy.wait_recv()
+    ab[:, 0] = (a1[y] + ra2[0]) + (ra2[1] + ra2[2])
+    for copy in second_b:
+        copy.wait_recv()
+    ab[:, 1] = (b1[x] + rb2[0]) + (rb2[1] + rb2[2])
+    last = [send(ab.at[p], rz.at[d], 16 + d, {AXIS_Z: p}) for d, p in enumerate(z_peers)]
+    g = [spacing * (miller[a].astype(jnp.float32) + kpoint[a]) for a in range(3)]
+    for copy in last:
+        copy.wait_recv()
+    weight = ab[z]
+    for d in range(7):
+        weight = weight + rz[d]
+    weight = weight.reshape(16, 128)
+    density[...] = 0.5 * (g[0] * g[0] + g[1] * g[1] + g[2] * g[2]) * weight
+    scaled = weight * (-1.0 / NPW)
+    rows = [
+        jnp.sum(scaled * g[a] * g[b], axis=0, keepdims=True)
+        for a, b in ((0, 0), (1, 1), (2, 2), (1, 2), (0, 2), (0, 1))
+    ]
+    tile[...] = jnp.concatenate(rows + [jnp.zeros((2, 128), jnp.float32)], axis=0)
+    for copy in pending:
+        copy.wait_send()
+
+
+def kinetic(coefficients, occupation, miller):
+    pairs = coefficients[0].reshape(2, 2, NPW // 128, 128).transpose(0, 2, 1, 3).reshape(2, NPW // 64, 128)
+    f32 = jnp.float32
+    vmem = pl.BlockSpec(memory_space=pltpu.VMEM)
+    return pl.pallas_call(
+        kinetic_kernel,
+        out_shape=(jax.ShapeDtypeStruct((16, 128), f32), jax.ShapeDtypeStruct((8, 128), f32)),
+        in_specs=[pl.BlockSpec(memory_space=pltpu.SMEM), vmem, vmem],
+        out_specs=(vmem, vmem),
+        scratch_shapes=[
+            pltpu.VMEM((64, 2, 32, 128), f32),
+            pltpu.VMEM((64, 32, 128), f32),
+            pltpu.VMEM((4, 32, 8, 128), f32),
+            pltpu.VMEM((4, 32, 8, 128), f32),
+            pltpu.VMEM((3, 32, 8, 128), f32),
+            pltpu.VMEM((3, 32, 8, 128), f32),
+            pltpu.VMEM((4, 8, 8, 128), f32),
+            pltpu.VMEM((4, 8, 8, 128), f32),
+            pltpu.VMEM((3, 8, 8, 128), f32),
+            pltpu.VMEM((3, 8, 8, 128), f32),
+            pltpu.VMEM((8, 2, 8, 128), f32),
+            pltpu.VMEM((7, 2, 8, 128), f32),
+            pltpu.VMEM((128, 128), f32),
+            pltpu.SemaphoreType.DMA((23,)),
+            pltpu.SemaphoreType.DMA((23,)),
+        ],
+        compiler_params=pltpu.CompilerParams(collective_id=0, has_side_effects=True),
+    )(occupation, pairs, miller.reshape(3, 16, 128))
+
+
+def total_kernel(tile, out, rz, ry, rx, held, ssem, rsem):
+    x, z, y, c = place()
+    stages = (
+        (rz, z, [(lax.rem(z + d, 8), {AXIS_Z: lax.rem(z + d, 8)}) for d in range(1, 8)], 8),
+        (ry, y, [(lax.rem(y + d, 4), {AXIS_Y: lax.rem(y + d, 4)}) for d in range(1, 4)], 4),
+        (rx, x * 2 + c, [
+            (None, {**at_x(lax.rem(x + d // 2, 4)), AXIS_C: lax.rem(c + d % 2, 2)}) for d in range(1, 8)
+        ], 8),
+    )
+    greet([peer for stage in stages for _, peer in stage[2]])
+    pending, k = [], 0
+    held[0] = tile[...]
+    for at, (slots, me, peers, count) in enumerate(stages):
+        copies = []
+        for _, peer in peers:
+            copy = pltpu.make_async_remote_copy(
+                src_ref=held.at[at], dst_ref=slots.at[me], send_sem=ssem.at[k], recv_sem=rsem.at[k],
+                device_id=peer, device_id_type=MESH,
+            )
+            copy.start()
+            copies.append(copy)
+            k += 1
+        slots[me] = held[at]
+        for copy in copies:
+            copy.wait_recv()
+        pending += copies
+        subtotal = slots[0]
+        for j in range(1, count):
+            subtotal = subtotal + slots[j]
+        held[at + 1] = subtotal
+    for a in range(6):
+        out[a] = jnp.sum(subtotal[a : a + 1, :])
+    for copy in pending:
+        copy.wait_send()
+
+
+def total(tile):
+    f32 = jnp.float32
+    return pl.pallas_call(
+        total_kernel,
+        out_shape=jax.ShapeDtypeStruct((6,), f32),
+        in_specs=[pl.BlockSpec(memory_space=pltpu.VMEM)],
+        out_specs=pl.BlockSpec(memory_space=pltpu.SMEM),
+        scratch_shapes=[
+            pltpu.VMEM((8, 8, 128), f32),
+            pltpu.VMEM((4, 8, 128), f32),
+            pltpu.VMEM((8, 8, 128), f32),
+            pltpu.VMEM((4, 8, 128), f32),
+            pltpu.SemaphoreType.DMA((17,)),
+            pltpu.SemaphoreType.DMA((17,)),
+        ],
+        compiler_params=pltpu.CompilerParams(collective_id=1, has_side_effects=True),
+    )(tile)
+
+
 def shards(coefficients, occupation, miller, density, local_factor):
     highest = lax.Precision.HIGHEST
-    weights = occupation.astype(jnp.float32) / occupation_unit
-    piece = coefficients.astype(jnp.float32)
-    squares = piece[0, 0] * piece[0, 0] + piece[0, 1] * piece[0, 1]
-    kinetic_weight = lax.psum_scatter(
-        jnp.dot(weights[0], squares, precision=highest), BAND_SPIN, scatter_dimension=0, tiled=True
-    )
-    kvec = jnp.array(kpoint, jnp.float32)
-    gvec = spacing * (miller.astype(jnp.float32) + kvec[:, None])
-    kinetic_density = 0.5 * (gvec[0] ** 2 + gvec[1] ** 2 + gvec[2] ** 2) * kinetic_weight
-    kinetic_stress = -six_sums(kinetic_weight, gvec[0], gvec[1], gvec[2]) / NPW
+    kinetic_density, tile = kinetic(coefficients, occupation, miller)
     band_devices = lax.axis_size(BAND)
     cell_count = density.shape[1] * band_devices * density.shape[2] * density.shape[3]
     deriv_x = derivative_table(NX)
@@ -159,9 +341,9 @@
     local_weight = 2.0 * (total_real * local_factor[0] + total_imag * local_factor[1])
     local_stress = six_sums(local_weight, freq_x, freq_y, freq_z)
     spin_share = 1.0 / lax.axis_size("spin")
-    partial_stress = kinetic_stress + spin_share * (hartree_stress + local_stress) + xc_stress
-    stress = by_axis(partial_stress, BAND_SPIN)
-    return (stress, kinetic_density, gradient_square)
+    partial_stress = spin_share * (hartree_stress + local_stress) + xc_stress
+    stress = total(tile + jnp.pad(partial_stress[:, None], ((0, 2), (0, 127))))
+    return (stress, kinetic_density.reshape(-1), gradient_square)
 
 
 def solution(mesh):

time: 369 us -> 130 us (0.35)
  waiting for transfers between devices: 219 us -> 15.5 us
  Pallas kernels: 0 us -> 43.8 us
  blocking collectives: 40 us -> 0 us
  matrix products: 31.6 us -> 14.6 us
  between operations: 16 us -> 2.84 us
  other arithmetic: 11.1 us -> 5.05 us
    unnamed x2 -> x0, waiting for transfers between devices: 203 us -> none
    pallas_call x0 -> x2, Pallas kernels: none -> 43.8 us  [the longest x1 29.4 us: kinetic(): pl.pallas_call(kinetic_kernel, out_shape=(jax.ShapeDtypeStruct((16, 128),...]
    psum x5 -> x0, blocking collectives: 40 us -> none  [by_axis(): shard = lax.psum(shard, axis)]
    dot_general x1 -> x0, matrix products: 17 us -> none  [shards(): jnp.dot(weights[0], squares, precision=highest)]
    convert_element_type x1 -> x0, other arithmetic: 4.73 us -> none  [shards(): piece = coefficients.astype(jnp.float32)]
    another operation x4 -> x3, local copies, waits for them, and re-layouts: 15.1 us -> 11.5 us  [six_sums(): jnp.stack([jnp.sum(weighting * first_axis * first_axis), jnp.sum(weightin...]
  transfers between devices with their start and end apart: 4 -> 3, of which waited for: 3 -> 2; matrix products, arithmetic and copies ran while one was open for 13% -> 6% of each run, Pallas kernels for 0% -> 23%
where the time goes in v1:
time: 130 us; the launch traced here: 129 us
  Pallas kernels  43.8 us (34%)
  starting transfers between devices  28.6 us (22%)
  local copies, waits for them, and re-layouts  18.6 us (14%)
  waiting for transfers between devices  15.5 us (12%)
  matrix products  14.6 us (11%)
  other arithmetic  5.05 us (4%)
  between operations  2.84 us (2%)
    pallas_call x1, Pallas kernels, kinetic(): pl.pallas_call(kinetic_kernel, out_shape=(jax.ShapeDtypeStruct((16, 128),...  29.4 us
    all_to_all x1, starting transfers between devices, sent_together(): lax.all_to_all(both, axis, split_axis=split_dim, concat_axis=concat_dim,...  14.9 us
    pallas_call x1, Pallas kernels, total(): pl.pallas_call(total_kernel, out_shape=jax.ShapeDtypeStruct((6,), f32), i...  14.5 us
    all_to_all x1, waiting for transfers between devices, shards(): lax.all_to_all(gradz_col, BAND, split_axis=1, concat_axis=2, tiled=True)  12.4 us
    another operation x3, local copies, waits for them, and re-layouts, six_sums(): jnp.stack([jnp.sum(weighting * first_axis * first_axis), jnp.sum(weightin...  11.5 us
    all_to_all x1, starting transfers between devices, shards(): lax.all_to_all(gradz_col, BAND, split_axis=1, concat_axis=2, tiled=True)  10.2 us
    all_to_all x1, starting transfers between devices, sent_to_all(): lax.all_to_all(jnp.broadcast_to(shard[None], (length, *shard.shape)), axi...  3.49 us
    unnamed x16, local copies, waits for them, and re-layouts  3.43 us
  transfers between devices with their start and end apart: 3, of which 2 were waited for; matrix products, arithmetic and copies ran while one was open for 6% of the time, Pallas kernels for 23%

profile of v1, /device:TPU:1, one launch (start us, length us, event | category | flops | bytes accessed | tf_op | source)
XLA Modules:
  0.0 129.0 jit_solution(5563810904488676287)
XLA Ops:
  0.6 0.0 copy-start
  0.6 0.0 copy-start.2
  0.7 1.4 %fusion.6 = f32[2,128,128]{1,2,0:T(8,128)S(1)} fusion(f32[1,2,128,128]{3,2,1,0:T(8,128)} %param.9), kind=kOutput, calls=%fused_computation.13 | convolution fusion | flops 50593792 | bytes 262144 | tf_op jit(solution)/shard_map/mj,szxj->szxm/dot_general | solution.py:308
  2.1 1.4 %convolution_bitcast_fusion.2 = f32[2,128,128]{1,2,0:T(8,128)S(1)} fusion(f32[1,2,128,128]{3,2,1,0:T(8,128)} %param.9), kind=kOutput, calls=%fused_computation.14 | convolution fusion | flops 50561024 | bytes 262144 | tf_op jit(solution)/shard_map/mj,szxj->szxm/dot_general | solution.py:307
  3.5 1.0 copy.41
  4.5 0.0 copy-start.1
  4.5 0.5 fusion.85
  5.1 0.5 fusion.87
  5.6 0.5 fusion.4
  6.1 0.5 fusion.5
  6.7 0.9 copy.42
  7.6 14.9 %all-to-all-start = ((f32[3,2,128,128]{3,1,0,2:T(2,128)}), f32[3,2,128,128]{3,1,0,2:T(2,128)S(1)}, u32[]{:S(2)}, u32[]{:S(2)}) async-start(f32[3,2,128,128]{3,1,0,2:T(2,128)} %copy.42), calls=%async_computation | async-start | bytes 786432 | tf_op jit(solution)/shard_map/all_to_all | solution.py:25
  22.5 0.7 dynamic_slice.3
  24.4 0.0 copy-done
  24.4 0.0 copy-done.2
  24.4 0.6 copy.60
  25.0 29.4 %shard_map.85 = (f32[16,128]{1,0:T(8,128)}, f32[8,128]{1,0:T(8,128)}) custom-call(s32[1,2]{1,0:T(1,128)} %occ.1, bf16[2,8192,128]{2,1,0:T(8,128)(2,1)} %bitcast.171, s32[3,16,128]{2,1,0:T(8,128)} %bitcast.182), custom_call_target="tpu_custom_call" | custom-call | tf_op jit(solution)/shard_map/pallas_call | solution.py:213
  55.1 0.0 copy-done.1
  55.1 0.6 convolution_bitcast_fusion.1
  55.7 0.0 all-to-all-done
  55.7 0.1 fusion.185
  55.8 1.6 %fusion.64 = f32[256,128]{1,0:T(8,128)S(1)} fusion(f32[256,128]{1,0:T(8,128)S(1)} %bitcast.178), kind=kOutput, calls=%fused_computation.109 | convolution fusion | flops 101580800 | bytes 262144 | tf_op jit(solution)/shard_map/mj,jxy->mxy/dot_general | solution.py:320
  57.4 1.6 %fusion.62 = f32[256,128]{1,0:T(8,128)S(1)} fusion(f32[256,128]{1,0:T(8,128)S(1)} %bitcast.180), kind=kOutput, calls=%fused_computation.108 | convolution fusion | flops 101580800 | bytes 262144 | tf_op jit(solution)/shard_map/mj,jxy->mxy/dot_general | solution.py:324
  59.0 1.6 %fusion.3 = f32[32768]{0:T(1024)S(1)} fusion(f32[256,128]{1,0:T(8,128)S(1)} %fusion.64, f32[256,128]{1,0:T(8,128)S(1)} %bitcast.181), kind=kOutput, calls=%fused_computation.6 | convolution fusion | flops 101646336 | bytes 393216 | tf_op jit(solution)/shard_map/mj,jxy->mxy/dot_general | solution.py:321
  60.5 1.6 %fusion.1 = f32[32768]{0:T(1024)S(1)} fusion(f32[256,128]{1,0:T(8,128)S(1)} %fusion.62, f32[256,128]{1,0:T(8,128)S(1)} %bitcast.179), kind=kOutput, calls=%fused_computation.3 | convolution fusion | flops 101646336 | bytes 393216 | tf_op jit(solution)/shard_map/mj,jxy->mxy/dot_general | solution.py:325
  62.1 1.6 %convolution_bitcast_fusion = f32[1,256,1,128]{1,3,2,0:T(8,128)S(1)} fusion(f32[256,128]{1,0:T(8,128)S(1)} %bitcast.177), kind=kOutput, calls=%fused_computation | convolution fusion | flops 102891520 | bytes 262144 | tf_op jit(solution)/shard_map/ik,skxy->sixy/dot_general | solution.py:316
  63.7 0.0 copy-start.5
  63.7 0.0 copy-start.4
  63.7 0.8 copy.46
  64.5 10.2 %all-to-all-start.2 = ((f32[1,256,1,128]{3,2,0,1:T(1,128)}), f32[1,256,1,128]{3,2,0,1:T(1,128)S(1)}, u32[]{:S(2)}, u32[]{:S(2)}) async-start(f32[1,256,1,128]{3,2,0,1:T(1,128)} %copy.46), calls=%async_computation.2 | async-start | bytes 262144 | tf_op jit(solution)/shard_map/all_to_all | solution.py:317
  74.7 12.4 %all-to-all-done.2 = f32[1,256,1,128]{3,2,0,1:T(1,128)S(1)} async-done(((f32[1,256,1,128]{3,2,0,1:T(1,128)}), f32[1,256,1,128]{3,2,0,1:T(1,128)S(1)}, u32[]{:S(2)}, u32[]{:S(2)}) %all-to-all-start.2) | async-done | bytes 131104 | tf_op jit(solution)/shard_map/all_to_all | solution.py:317
  87.1 1.1 broadcast_in_dim.18
  88.1 3.5 %all-to-all-start.1 = ((f32[2,1,65536]{2,1,0:T(1,128)}), f32[2,1,65536]{2,1,0:T(1,128)S(1)}, u32[]{:S(2)}, u32[]{:S(2)}) async-start(f32[2,1,65536]{2,1,0:T(1,128)} %broadcast_in_dim.18), calls=%async_computation.1 | async-start | bytes 1048576 | tf_op jit(solution)/shard_map/all_to_all | solution.py:37
  91.6 1.3 %fusion.36 = (f32[1,2,128,128]{3,2,1,0:T(8,128)S(1)}, f32[1,2,128,128]{3,2,1,0:T(8,128)}, f32[128,2,128]{0,2,1:T(8,128)S(1)}) fusion(f32[1,2,128,128]{3,2,1,0:T(8,128)S(1)} %copy-done.1, f32[1,128,2,1,128]{4,2,1,3,0:T(2,128)S(1)} %bitcast.174, f32[1,2,128,128]{3,2,1,0:T(8,128)S(1)} %convolution_bitcast_fusion.1), kind=kOutput, calls=%fused_computation.57 | convolution fusion | flops 51249152 | bytes 786432 | tf_op jit(solution)/shard_map/ik,szxk->szxi/dot_general | solution.py:306
  93.0 0.8 fusion.41
  93.8 3.9 %stack.83 = f32[6]{0:T(128)S(1)} concatenate(f32[1]{0:T(128)} %bitcast.50, f32[1]{0:T(128)} %bitcast.52, f32[1]{0:T(128)} %bitcast.54, f32[1]{0:T(128)} %bitcast.55, f32[1]{0:T(128)} %bitcast.56, f32[1]{0:T(128)} %bitcast.58), dimensions={0} | concatenate | bytes 48 | tf_op jit(solution)/shard_map/stack | solution.py:81
  97.6 3.1 %all-to-all-done.1 = f32[2,1,65536]{2,1,0:T(1,128)S(1)} async-done(((f32[2,1,65536]{2,1,0:T(1,128)}), f32[2,1,65536]{2,1,0:T(1,128)S(1)}, u32[]{:S(2)}, u32[]{:S(2)}) %all-to-all-start.1) | async-done | bytes 524320 | tf_op jit(solution)/shard_map/all_to_all | solution.py:37
  100.7 0.7 reduce_sum.180
  101.5 0.7 fusion.98
  102.2 1.5 %multiply_reduce_fusion.2 = (f32[]{:T(128)}, f32[]{:T(128)}, f32[]{:T(128)}, f32[]{:T(128)}, f32[]{:T(128)}, /*index=5*/f32[]{:T(128)}, f32[]{:T(128)}, f32[]{:T...) fusion(f32[256,128]{1,0:T(8,128)S(1)} %get-tuple-element.38, f32[]{:T(128)S(6)} %mul.581, ...), kind=kLoop, calls=%fused_computation.91 | loop fusion | flops 983028 | bytes 265272 | tf_op jit(solution)/shard_map/reduce_sum | solution.py:87
  103.7 3.8 %stack.69 = f32[6]{0:T(128)S(1)} concatenate(f32[1]{0:T(128)} %bitcast.23, f32[1]{0:T(128)} %bitcast.24, f32[1]{0:T(128)} %bitcast.25, f32[1]{0:T(128)} %bitcast.26, f32[1]{0:T(128)} %bitcast.27, f32[1]{0:T(128)} %bitcast.28), dimensions={0} | concatenate | bytes 48 | tf_op jit(solution)/shard_map/stack | solution.py:81
  107.5 3.8 %stack.76 = f32[6]{0:T(128)S(1)} concatenate(f32[1]{0:T(128)} %bitcast.32, f32[1]{0:T(128)} %bitcast.33, f32[1]{0:T(128)} %bitcast.34, f32[1]{0:T(128)} %bitcast.35, f32[1]{0:T(128)} %bitcast.36, f32[1]{0:T(128)} %bitcast.37), dimensions={0} | concatenate | bytes 48 | tf_op jit(solution)/shard_map/stack | solution.py:81
  111.3 0.7 add_bitcast_fusion
  112.0 0.1 copy.48
  112.1 0.6 pad_add_fusion.tile
  112.7 14.5 %shard_map.86 = f32[6]{0:T(128)} custom-call(f32[8,128]{1,0:T(8,128)} %pad_add_fusion.tile), custom_call_target="tpu_custom_call" | custom-call | tf_op jit(solution)/shard_map/pallas_call | solution.py:277
  127.2 1.2 copy.63
  128.4 0.6 copy.64
  (11 shorter events, 0.1 us)
Async XLA Ops:
  0.6 23.8 %copy-start = (f32[2,256,1,128]{3,2,1,0:T(1,128)S(1)}, f32[2,256,1,128]{3,2,1,0:T(1,128)}, u32[]{:S(2)}) copy-start(f32[2,256,1,128]{3,2,1,0:T(1,128)} %param.10) | copy-start | bytes 786436
  0.6 23.8 %copy-start.2 = (s32[3,2048]{1,0:T(4,128)S(1)}, s32[3,2048]{1,0:T(4,128)}, u32[]{:S(2)}) copy-start(s32[3,2048]{1,0:T(4,128)} %param.8) | copy-start | bytes 73732
  4.5 50.6 %copy-start.1 = (f32[1,2,128,128]{3,2,1,0:T(8,128)S(1)}, f32[1,2,128,128]{3,2,1,0:T(8,128)}, u32[]{:S(2)}) copy-start(f32[1,2,128,128]{3,2,1,0:T(8,128)} %param.9) | copy-start | bytes 393220
  7.6 48.1 %all-to-all-start = ((f32[3,2,128,128]{3,1,0,2:T(2,128)}), f32[3,2,128,128]{3,1,0,2:T(2,128)S(1)}, u32[]{:S(2)}, u32[]{:S(2)}) async-start(f32[3,2,128,128]{3,1,0,2:T(2,128)} %copy.42), calls=%async_computation | async-start | bytes 786432 | tf_op jit(solution)/shard_map/all_to_all | solution.py:25
  63.7 47.7 %copy-start.5 = (f32[6]{0:T(128)S(1)}, f32[6]{0:T(128)}, u32[]{:S(2)}) copy-start(f32[6]{0:T(128)} %constant.142.clone) | copy-start | bytes 76
  63.7 48.4 %copy-start.4 = (f32[8,128]{1,0:T(8,128)S(1)}, f32[8,128]{1,0:T(8,128)}, u32[]{:S(2)}) copy-start(f32[8,128]{1,0:T(8,128)} %get-tuple-element.5) | copy-start | bytes 12292
  63.7 64.7 %copy-start.3 = (f32[16,128]{1,0:T(8,128)S(1)}, f32[16,128]{1,0:T(8,128)}, u32[]{:S(2)}) copy-start(f32[16,128]{1,0:T(8,128)} %get-tuple-element.6) | copy-start | bytes 24580
  64.5 22.6 %all-to-all-start.2 = ((f32[1,256,1,128]{3,2,0,1:T(1,128)}), f32[1,256,1,128]{3,2,0,1:T(1,128)S(1)}, u32[]{:S(2)}, u32[]{:S(2)}) async-start(f32[1,256,1,128]{3,2,0,1:T(1,128)} %copy.46), calls=%async_computation.2 | async-start | bytes 262144 | tf_op jit(solution)/shard_map/all_to_all | solution.py:317
  88.1 12.6 %all-to-all-start.1 = ((f32[2,1,65536]{2,1,0:T(1,128)}), f32[2,1,65536]{2,1,0:T(1,128)S(1)}, u32[]{:S(2)}, u32[]{:S(2)}) async-start(f32[2,1,65536]{2,1,0:T(1,128)} %broadcast_in_dim.18), calls=%async_computation.1 | async-start | bytes 1048576 | tf_op jit(solution)/shard_map/all_to_all | solution.py:37

commit v2 on v1

--- a/solution.py
+++ b/solution.py
@@ -1,3 +1,5 @@
+import functools
+
 import jax
 import jax.numpy as jnp
 from jax import lax
@@ -17,19 +19,6 @@
 occupation_unit = 1000.0
 kpoint = (0.25, 0.125, 0.375)
 spacing = 0.25
-
-
-def sent_together(arrays, axis, split_dim, concat_dim, along):
-    both = jnp.concatenate(arrays, axis=along)
-    result, at, gathered = (
-        lax.all_to_all(both, axis, split_axis=split_dim, concat_axis=concat_dim, tiled=True),
-        0,
-        [],
-    )
-    for a in arrays:
-        gathered.append(lax.slice_in_dim(result, at, at + a.shape[along], axis=along))
-        at += a.shape[along]
-    return tuple(gathered)
 
 
 def sent_to_all(shard, axis):
@@ -291,6 +280,63 @@
     )(tile)
 
 
+def exchange_kernel(count, *refs):
+    outgoing, incoming = refs[:count], refs[count : 2 * count]
+    far, ssem, rsem = refs[2 * count :]
+    x, z, y, c = place()
+    x_lo = lax.rem(x, 2)
+    me = ((x_lo * 8 + z) * 4 + y) * 2 + c
+    z_peers = [{AXIS_Z: lax.rem(z + d, 8)} for d in range(1, 8)]
+    plane = [
+        {AXIS_XLO: lax.rem(x_lo + d // 8, 2), AXIS_Y: lax.rem(y + d // 2, 4), AXIS_C: lax.rem(c + d, 2)}
+        for d in range(1, 16)
+    ]
+    greet(z_peers + plane)
+    for peer in z_peers:
+        pl.semaphore_signal(far, inc=1, device_id=peer, device_id_type=MESH)
+    pl.semaphore_wait(far, 7)
+
+    def push(d, carry):
+        t = lax.rem(me + d, 128)
+        peer = {AXIS_XLO: t // 64, AXIS_Z: lax.rem(t // 8, 8), AXIS_Y: lax.rem(t // 2, 4), AXIS_C: lax.rem(t, 2)}
+        for k in range(count):
+            pltpu.make_async_remote_copy(
+                src_ref=outgoing[k].at[t], dst_ref=incoming[k].at[me], send_sem=ssem.at[k], recv_sem=rsem.at[k],
+                device_id=peer, device_id_type=MESH,
+            ).start()
+        return carry
+
+    lax.fori_loop(1, 128, push, 0)
+    for k in range(count):
+        incoming[k][me] = outgoing[k][me]
+    for k in range(count):
+        bulk = incoming[k].at[pl.ds(0, 127)]
+        pltpu.make_async_copy(bulk, bulk, rsem.at[k]).wait()
+        pltpu.make_async_copy(bulk, bulk, ssem.at[k]).wait()
+
+
+def exchange(arrays, collective_id):
+    count = len(arrays)
+    vmem = pl.BlockSpec(memory_space=pltpu.VMEM)
+    return pl.pallas_call(
+        functools.partial(exchange_kernel, count),
+        out_shape=tuple(jax.ShapeDtypeStruct((128, 2, 128), jnp.float32) for _ in arrays),
+        in_specs=[vmem] * count,
+        out_specs=(vmem,) * count,
+        scratch_shapes=[
+            pltpu.SemaphoreType.REGULAR,
+            pltpu.SemaphoreType.DMA((count,)),
+            pltpu.SemaphoreType.DMA((count,)),
+        ],
+        compiler_params=pltpu.CompilerParams(collective_id=collective_id, has_side_effects=True),
+    )(*arrays)
+
+
+def to_columns(arrays, collective_id):
+    gathered = exchange([a[0].transpose(1, 0, 2) for a in arrays], collective_id)
+    return tuple(g.reshape(1, NZ, 1, NY) for g in gathered)
+
+
 def shards(coefficients, occupation, miller, density, local_factor):
     highest = lax.Precision.HIGHEST
     kinetic_density, tile = kinetic(coefficients, occupation, miller)
@@ -312,9 +358,9 @@
     plane_imag = jnp.einsum("mj,szjy->szmy", cosine_x, along_imag, precision=highest) - jnp.einsum(
         "mj,szjy->szmy", sine_x, along_real, precision=highest
     )
-    dens_col, real_col, imag_col = sent_together((density, plane_real, plane_imag), BAND, 2, 1, 0)
+    dens_col, real_col, imag_col = to_columns((density, plane_real, plane_imag), 2)
     gradz_col = jnp.einsum("ik,skxy->sixy", deriv_z, dens_col, precision=highest)
-    grad_z = lax.all_to_all(gradz_col, BAND, split_axis=1, concat_axis=2, tiled=True)
+    grad_z = exchange([gradz_col.reshape(128, 2, 128)], 3)[0].transpose(1, 0, 2)[None]
     gradient_square, xc_stress = xc_terms(density, grad_x, grad_y, grad_z, cell_count)
     spec_real = (
         jnp.einsum("mj,jxy->mxy", cosine_z, real_col[0], precision=highest)

time: 130 us -> 139 us (1.069)
  Pallas kernels: 43.8 us -> 87.9 us
  starting transfers between devices: 28.6 us -> 4.05 us
  waiting for transfers between devices: 15.5 us -> 0.01 us
  other arithmetic: 5.05 us -> 8.58 us
  local copies, waits for them, and re-layouts: 18.6 us -> 20.5 us
    pallas_call x0 -> x2, Pallas kernels: none -> 42.9 us  [exchange(): pl.pallas_call(functools.partial(exchange_kernel, count), out_shape=tuple...]
    all_to_all x2 -> x0, starting transfers between devices: 25.1 us -> none  [the longest x1 14.9 us: sent_together(): lax.all_to_all(both, axis, split_axis=split_dim, concat_axis=concat_dim,...]
    all_to_all x2 -> x0, waiting for transfers between devices: 12.4 us -> none  [the longest x1 12.4 us: shards(): lax.all_to_all(gradz_col, BAND, split_axis=1, concat_axis=2, tiled=True)]
    pallas_call x1, Pallas kernels: 14.5 us -> 17.9 us  [total(): pl.pallas_call(total_kernel, out_shape=jax.ShapeDtypeStruct((6,), f32), i...]
    all_to_all x1, waiting for transfers between devices: 3.09 us -> 0.01 us  [sent_to_all(): lax.all_to_all(jnp.broadcast_to(shard[None], (length, *shard.shape)), axi...]
    pallas_call x1, Pallas kernels: 29.4 us -> 27 us  [kinetic(): pl.pallas_call(kinetic_kernel, out_shape=(jax.ShapeDtypeStruct((16, 128),...]
    div x0 -> x1, other arithmetic: none -> 1.71 us  [xc_terms(): dens_part ** (-1.0 / 3.0)]
    unnamed x16 -> x19, local copies, waits for them, and re-layouts: 3.43 us -> 4.81 us
  transfers between devices with their start and end apart: 3 -> 1, of which waited for: 2 -> 0; matrix products, arithmetic and copies ran while one was open for 6% -> 9% of each run, Pallas kernels for 23% -> 31%
where the time goes in v2:
time: 139 us
  Pallas kernels  87.9 us (63%)
  local copies, waits for them, and re-layouts  20.5 us (15%)
  matrix products  14.8 us (11%)
  other arithmetic  8.58 us (6%)
  starting transfers between devices  4.05 us (3%)
  between operations  2.79 us (2%)
    pallas_call x2, Pallas kernels, exchange(): pl.pallas_call(functools.partial(exchange_kernel, count), out_shape=tuple...  42.9 us
    pallas_call x1, Pallas kernels, kinetic(): pl.pallas_call(kinetic_kernel, out_shape=(jax.ShapeDtypeStruct((16, 128),...  27 us
    pallas_call x1, Pallas kernels, total(): pl.pallas_call(total_kernel, out_shape=jax.ShapeDtypeStruct((6,), f32), i...  17.9 us
    another operation x3, local copies, waits for them, and re-layouts, six_sums(): jnp.stack([jnp.sum(weighting * first_axis * first_axis), jnp.sum(weightin...  11.5 us
    unnamed x19, local copies, waits for them, and re-layouts  4.81 us
    all_to_all x1, starting transfers between devices, sent_to_all(): lax.all_to_all(jnp.broadcast_to(shard[None], (length, *shard.shape)), axi...  4.05 us
  transfers between devices with their start and end apart: 1, of which 0 were waited for; matrix products, arithmetic and copies ran while one was open for 9% of the time, Pallas kernels for 31%

profile of v2, /device:TPU:1, one launch (start us, length us, event | category | flops | bytes accessed | tf_op | source)
XLA Modules:
  0.0 138.5 jit_solution(9399707922625057136)
XLA Ops:
  0.6 1.0 copy.111
  1.6 0.0 copy-start
  1.7 0.5 convolution_bitcast_fusion.1
  2.2 0.5 fusion.4
  2.7 0.5 fusion.86
  3.2 0.5 fusion.84
  3.7 0.5 convolution_add_fusion.1
  4.2 0.7 copy.71
  5.0 0.5 convolution_subtract_fusion.1
  5.5 0.8 copy.72
  6.2 0.0 copy-done
  6.3 26.6 %shard_map.86 = (f32[128,2,128]{2,1,0:T(2,128)}, f32[128,2,128]{2,1,0:T(2,128)}, f32[128,2,128]{2,1,0:T(2,128)}) custom-call(f32[128,2,128]{2,1,0:T(2,128)} %bitcast.186, f32[128,2,128]{2,1,0:T(2,128)} %bitcast.189, f32[128,2,128]{2,1,0:T(2,128)} %bitcast.190), custom_call_target="tpu_custom_call" | custom-call | tf_op jit(solution)/shard_map/pallas_call | solution.py:321
  32.8 0.0 copy-start.1
  32.8 0.0 copy-start.6
  32.9 2.3 %fusion.55 = f32[256,128]{1,0:T(8,128)S(1)} fusion(f32[256,128]{1,0:T(8,128)} %bitcast.198), kind=kOutput, calls=%fused_computation.101 | convolution fusion | flops 101580800 | bytes 262144 | tf_op jit(solution)/shard_map/mj,jxy->mxy/dot_general | solution.py:370
  35.1 2.2 %fusion.57 = f32[256,128]{1,0:T(8,128)S(1)} fusion(f32[256,128]{1,0:T(8,128)} %bitcast.200), kind=kOutput, calls=%fused_computation.102 | convolution fusion | flops 101580800 | bytes 262144 | tf_op jit(solution)/shard_map/mj,jxy->mxy/dot_general | solution.py:366
  37.4 2.2 %fusion.1 = f32[32768]{0:T(1024)S(1)} fusion(f32[256,128]{1,0:T(8,128)S(1)} %fusion.55, f32[256,128]{1,0:T(8,128)} %bitcast.201), kind=kOutput, calls=%fused_computation.3 | convolution fusion | flops 101646336 | bytes 393216 | tf_op jit(solution)/shard_map/mj,jxy->mxy/dot_general | solution.py:371
  39.6 2.2 %fusion.3 = f32[32768]{0:T(1024)S(1)} fusion(f32[256,128]{1,0:T(8,128)S(1)} %fusion.57, f32[256,128]{1,0:T(8,128)} %bitcast.199), kind=kOutput, calls=%fused_computation.6 | convolution fusion | flops 101646336 | bytes 393216 | tf_op jit(solution)/shard_map/mj,jxy->mxy/dot_general | solution.py:367
  41.9 0.0 copy-start.2
  41.9 1.1 broadcast_in_dim.20
  43.0 4.0 %all-to-all-start = ((f32[2,1,65536]{2,1,0:T(1,128)}), f32[2,1,65536]{2,1,0:T(1,128)S(1)}, u32[]{:S(2)}, u32[]{:S(2)}) async-start(f32[2,1,65536]{2,1,0:T(1,128)} %broadcast_in_dim.20), calls=%async_computation | async-start | bytes 1048576 | tf_op jit(solution)/shard_map/all_to_all | solution.py:26
  47.0 0.6 fusion.61
  47.6 0.6 fusion.63
  48.2 0.1 copy.79
  48.3 1.6 %convolution_bitcast_fusion = f32[1,256,1,128]{1,3,2,0:T(8,128)S(1)} fusion(f32[256,128]{1,0:T(8,128)S(1)} %bitcast.197), kind=kOutput, calls=%fused_computation | convolution fusion | flops 102891520 | bytes 262144 | tf_op jit(solution)/shard_map/ik,skxy->sixy/dot_general | solution.py:362
  49.9 0.8 copy.80
  50.7 16.3 %shard_map.87 = f32[128,2,128]{2,1,0:T(2,128)} custom-call(f32[128,2,128]{2,1,0:T(2,128)} %bitcast.191), custom_call_target="tpu_custom_call" | custom-call | tf_op jit(solution)/shard_map/pallas_call | solution.py:321
  67.0 0.0 copy-done.2
  67.0 1.7 %add_divide_fusion = (f32[1,2,128,128]{3,1,2,0:T(2,128)S(1)}, f32[1,2,128,128]{3,1,2,0:T(2,128)S(1)}) fusion(f32[1,2,128,128]{3,2,1,0:T(8,128)S(1)} %copy-done.2, f32[128,2,128]{2,1,0:T(2,128)} %shard_map.87, f32[128,2,128]{0,1,2:T(2,128)S(1)} %copy.79, f32[128,2,128]{2,0,1:T(8,128)S(1)} %fusion.63), kind=kLoop, calls=%fused_computation.75 | loop fusion | flops 360448 | bytes 786432 | tf_op jit(solution)/shard_map/div | solution.py:84
  68.7 2.0 %fusion.40 = (f32[]{:T(128)}, f32[]{:T(128)}, f32[]{:T(128)}, f32[]{:T(128)}, f32[]{:T(128)}, /*index=5*/f32[]{:T(128)}) fusion(f32[128,2,128]{0,1,2:T(2,128)S(1)} %copy.79, f32[1,2,128,128]{3,1,2,0:T(2,128)S(1)} %get-tuple-element.49, f32[128,2,128]{2,0,1:T(8,128)S(1)} %fusion.63, f32[128,2,128]{2,1,0:T(2,128)} %shard_map.87), kind=kLoop, calls=%fused_computation.68 | loop fusion | flops 491514 | bytes 524312 | tf_op jit(solution)/shard_map/reduce_sum | solution.py:77
  70.7 0.7 dynamic_slice.3
  72.6 0.6 copy.112
  73.2 0.0 copy-done.3
  73.3 27.0 %shard_map.85 = (f32[16,128]{1,0:T(8,128)}, f32[8,128]{1,0:T(8,128)}) custom-call(s32[1,2]{1,0:T(1,128)} %occ.1, bf16[2,8192,128]{2,1,0:T(8,128)(2,1)} %bitcast.183, s32[3,16,128]{2,1,0:T(8,128)} %bitcast.194), custom_call_target="tpu_custom_call" | custom-call | tf_op jit(solution)/shard_map/pallas_call | solution.py:202
  100.3 0.7 copy.84
  101.6 3.8 %stack.83 = f32[6]{0:T(128)S(1)} concatenate(f32[1]{0:T(128)} %bitcast.52, f32[1]{0:T(128)} %bitcast.54, f32[1]{0:T(128)} %bitcast.56, f32[1]{0:T(128)} %bitcast.58, f32[1]{0:T(128)} %bitcast.59, f32[1]{0:T(128)} %bitcast.61), dimensions={0} | concatenate | bytes 48 | tf_op jit(solution)/shard_map/stack | solution.py:70
  105.4 0.0 all-to-all-done
  105.5 0.7 reduce_sum.180
  106.2 0.7 fusion.97
  106.9 1.5 %multiply_reduce_fusion.1 = (f32[]{:T(128)}, f32[]{:T(128)}, f32[]{:T(128)}, f32[]{:T(128)}, f32[]{:T(128)}, /*index=5*/f32[]{:T(128)}, f32[]{:T(128)}, f32[]{:T...) fusion(f32[256,128]{1,0:T(8,128)S(1)} %get-tuple-element.53, f32[]{:T(128)S(6)} %mul.576, ...), kind=kLoop, calls=%fused_computation.84 | loop fusion | flops 983028 | bytes 265272 | tf_op jit(solution)/shard_map/reduce_sum | solution.py:76
  108.4 3.8 %stack.76 = f32[6]{0:T(128)S(1)} concatenate(f32[1]{0:T(128)} %bitcast.34, f32[1]{0:T(128)} %bitcast.35, f32[1]{0:T(128)} %bitcast.36, f32[1]{0:T(128)} %bitcast.37, f32[1]{0:T(128)} %bitcast.38, f32[1]{0:T(128)} %bitcast.39), dimensions={0} | concatenate | bytes 48 | tf_op jit(solution)/shard_map/stack | solution.py:70
  112.3 3.8 %stack.69 = f32[6]{0:T(128)S(1)} concatenate(f32[1]{0:T(128)} %bitcast.25, f32[1]{0:T(128)} %bitcast.26, f32[1]{0:T(128)} %bitcast.27, f32[1]{0:T(128)} %bitcast.28, f32[1]{0:T(128)} %bitcast.29, f32[1]{0:T(128)} %bitcast.30), dimensions={0} | concatenate | bytes 48 | tf_op jit(solution)/shard_map/stack | solution.py:70
  116.1 0.7 add_bitcast_fusion
  116.7 0.1 copy.83
  116.8 1.3 pad_add_fusion.tile
  118.1 17.9 %shard_map.88 = f32[6]{0:T(128)} custom-call(f32[8,128]{1,0:T(8,128)} %pad_add_fusion.tile), custom_call_target="tpu_custom_call" | custom-call | tf_op jit(solution)/shard_map/pallas_call | solution.py:266
  136.0 1.2 copy.115
  137.2 1.3 copy.116
  (13 shorter events, 0.1 us)
Async XLA Ops:
  1.6 4.6 %copy-start = (f32[1,2,128,128]{3,1,2,0:T(2,128)}, f32[1,2,128,128]{3,1,2,0:T(2,128)S(1)}, u32[]{:S(2)}) copy-start(f32[1,2,128,128]{3,1,2,0:T(2,128)S(1)} %copy.111) | copy-start | bytes 393220
  32.8 14.2 %copy-start.1 = (f32[1,2,128,128]{3,1,2,0:T(2,128)S(1)}, f32[1,2,128,128]{3,1,2,0:T(2,128)}, u32[]{:S(2)}) copy-start(f32[1,2,128,128]{3,1,2,0:T(2,128)} %copy-done) | copy-start | bytes 393220
  32.8 15.5 %copy-start.6 = (f32[128,2,128]{2,1,0:T(2,128)S(1)}, f32[128,2,128]{2,1,0:T(2,128)}, u32[]{:S(2)}) copy-start(f32[128,2,128]{2,1,0:T(2,128)} %get-tuple-element.11) | copy-start | bytes 393220
  41.9 25.1 %copy-start.2 = (f32[1,2,128,128]{3,2,1,0:T(8,128)S(1)}, f32[1,2,128,128]{3,2,1,0:T(8,128)}, u32[]{:S(2)}) copy-start(f32[1,2,128,128]{3,2,1,0:T(8,128)} %param.9) | copy-start | bytes 393220
  43.0 29.7 %copy-start.4 = (s32[3,2048]{1,0:T(4,128)S(1)}, s32[3,2048]{1,0:T(4,128)}, u32[]{:S(2)}) copy-start(s32[3,2048]{1,0:T(4,128)} %param.8) | copy-start | bytes 73732
  43.0 30.3 %copy-start.3 = (f32[2,256,1,128]{3,2,1,0:T(1,128)S(1)}, f32[2,256,1,128]{3,2,1,0:T(1,128)}, u32[]{:S(2)}) copy-start(f32[2,256,1,128]{3,2,1,0:T(1,128)} %param.10) | copy-start | bytes 786436
  43.0 62.5 %all-to-all-start = ((f32[2,1,65536]{2,1,0:T(1,128)}), f32[2,1,65536]{2,1,0:T(1,128)S(1)}, u32[]{:S(2)}, u32[]{:S(2)}) async-start(f32[2,1,65536]{2,1,0:T(1,128)} %broadcast_in_dim.20), calls=%async_computation | async-start | bytes 1048576 | tf_op jit(solution)/shard_map/all_to_all | solution.py:26
  50.7 65.4 %copy-start.5 = (f32[6]{0:T(128)S(1)}, f32[6]{0:T(128)}, u32[]{:S(2)}) copy-start(f32[6]{0:T(128)} %constant.142.clone) | copy-start | bytes 76

commit v3 on v0

v3 whole, which is shorter than its diff:
```python
import jax
import jax.numpy as jnp
import numpy as np
from jax import lax
from jax.experimental import pallas as pl
from jax.experimental.pallas import tpu as pltpu
from jax.sharding import PartitionSpec as P

NPW = 524288
NX = 128
NY = 128
NZ = 256
CELLS = NX * NY * NZ
MESH = pl.DeviceIdType.MESH
F32, BF16 = jnp.float32, jnp.bfloat16

occupation_unit = 1000.0
kpoint = (0.25, 0.125, 0.375)
spacing = 0.25


def derivative_table(length):
    apart = np.arange(length)[:, None] - np.arange(length)[None, :]
    angles = np.pi / length * np.where(apart == 0, 1, apart)
    return np.where(apart == 0, 0.0, 0.5 * (1.0 - 2.0 * (apart % 2)) * np.cos(angles) / np.sin(angles))


def fourier_tables(length):
    index = np.arange(length)
    phases = (index[:, None] * index[None, :]) % length * (2.0 * np.pi / length)
    return np.cos(phases), np.sin(phases)


def halves(table):
    table = np.asarray(table, np.float32)
    high = table.astype(BF16)
    return np.stack([high, (table - high.astype(np.float32)).astype(BF16)])


def tables():
    cos_y, sin_y = fourier_tables(NY)
    cos_x, sin_x = fourier_tables(NX)
    cos_z, sin_z = fourier_tables(NZ)
    lo, hi = slice(0, 64), slice(64, 128)
    re, im = cos_y, -sin_y
    along_y = np.concatenate(
        [re[:, lo], im[:, lo], re[:, hi], im[:, hi], im[:, lo], -re[:, lo], im[:, hi], -re[:, hi], derivative_table(NY).T],
        axis=1,
    )
    along_x = np.concatenate([cos_x, sin_x], axis=1)
    along_z = np.concatenate([cos_z, sin_z], axis=1)
    return [halves(t) for t in (along_y, along_x, along_z, derivative_table(NX), derivative_table(NZ))]


def split(value):
    high = value.astype(BF16)
    return high, (value - high.astype(F32)).astype(BF16)


def product(left, right):
    def dot(a, b):
        return jnp.dot(a, b, preferred_element_type=F32)

    return dot(left[0], right[0]) + (dot(left[0], right[1]) + dot(left[1], right[0]))


def pair(table):
    return table[0], table[1]


def stress_kernel(
    occ, miller, coef_any, dens_any, factor_any, ty_any, tx_any, tz_any, dx_any, dz_any,
    stress, density_out, square_out,
    coef, dens, factor, ty, tx, tz, dx, dz,
    sn, rn, gz, rg, sp, rsp,
    part, twin, qa, qb, ra, rb, a1, b1, ra2, rb2, ab, rz, tmp,
    held, tot_z, tot_p,
    gradx, grady, far, lsem, ssem, rsem, bulk_s, bulk_r, tsem_s, tsem_r,
):
    band, s = lax.axis_index("band"), lax.axis_index("spin")
    x_lo, z, y, c = band // 64, lax.rem(band // 8, 8), lax.rem(band // 2, 4), lax.rem(band, 2)
    x = s * 2 + x_lo
    other = 1 - c

    def at(x_=None, z_=None, y_=None, c_=None):
        x_ = x if x_ is None else x_
        z_ = z if z_ is None else z_
        y_ = y if y_ is None else y_
        c_ = c if c_ is None else c_
        return {"band": ((lax.rem(x_, 2) * 8 + z_) * 4 + y_) * 2 + c_, "spin": x_ // 2}

    x_peers = [lax.rem(x + d, 4) for d in (1, 2, 3)]
    y_peers = [lax.rem(y + d, 4) for d in (1, 2, 3)]
    z_peers = [lax.rem(z + d, 8) for d in range(1, 8)]
    plane = [
        at(x_=lax.rem(x + d // 8, 4), y_=lax.rem(y + d // 2, 4), c_=lax.rem(c + d, 2)) for d in range(1, 32)
    ]

    locals_ = []
    for k, (src, dst) in enumerate(
        ((dens_any, dens), (ty_any, ty), (tx_any, tx), (dx_any, dx), (coef_any, coef), (dz_any, dz), (tz_any, tz), (factor_any, factor))
    ):
        copy = pltpu.make_async_copy(src, dst, lsem.at[k])
        copy.start()
        locals_.append(copy)
    load_dens, load_ty, load_tx, load_dx, load_coef, load_dz, load_tz, load_factor = locals_
    barrier = pltpu.get_barrier_semaphore()
    for p in z_peers:
        pl.semaphore_signal(barrier, inc=1, device_id=at(z_=p), device_id_type=MESH)
    for peer in plane:
        pl.semaphore_signal(barrier, inc=1, device_id=peer, device_id_type=MESH)

    pending = []

    def send(src, dst, k, peer):
        copy = pltpu.make_async_remote_copy(
            src_ref=src, dst_ref=dst, send_sem=ssem.at[k], recv_sem=rsem.at[k], device_id=peer, device_id_type=MESH
        )
        copy.start()
        pending.append(copy)
        return copy

    load_dens.wait()
    sn_flat = sn.reshape(256, 128)
    for zz in range(2):
        sn_flat[pl.ds(zz, 128, stride=2), :] = dens[zz]

    load_coef.wait()
    w0 = jnp.full((64, 128), occ[0, 0].astype(F32)) / occupation_unit
    w1 = jnp.full((64, 128), occ[0, 1].astype(F32)) / occupation_unit

    def squares(i, carry):
        rows = pl.ds(pl.multiple_of(i * 128, 128), 128)
        re = coef[0, rows, :].astype(F32)
        im = coef[1, rows, :].astype(F32)
        tmp[...] = re * re + im * im
        both = w0 * tmp[pl.ds(0, 64, stride=2), :] + w1 * tmp[pl.ds(1, 64, stride=2), :]
        part[i] = both.reshape(2, 32, 128)
        return carry

    lax.fori_loop(0, 64, squares, 0)

    pl.semaphore_wait(barrier, 38)
    for p in z_peers:
        pl.semaphore_signal(far, inc=1, device_id=at(z_=p), device_id_type=MESH)
    twins = [
        send(part.at[pl.ds(q * 16, 16), other], twin.at[pl.ds(q * 16, 16)], q, at(c_=other)) for q in range(4)
    ]

    load_ty.wait()
    load_tx.wait()
    load_dx.wait()
    rows = split(dens[...].reshape(256, 128))
    from_y = product(rows, pair(ty))
    wide = split(jnp.concatenate([dens[0], dens[1]], axis=1))
    gx = product(pair(dx), wide)
    sp_flat = sp.reshape(512, 128)
    for zz in range(2):
        mine = from_y[zz * 128 : zz * 128 + 128]
        grady[zz] = mine[:, 512:640]
        gradx[zz] = gx[:, zz * 128 : zz * 128 + 128]
        turned = product(pair(tx), split(jnp.concatenate([mine[:, 0:256], mine[:, 256:512]], axis=0)))
        for half in range(2):
            sp_flat[pl.ds(half * 256 + zz, 128, stride=2), :] = turned[:, half * 128 : half * 128 + 128]

    pl.semaphore_wait(far, 7)

    def push_density(d, carry):
        t = lax.rem(band + d, 128)
        pltpu.make_async_remote_copy(
            src_ref=sn.at[t], dst_ref=rn.at[band], send_sem=bulk_s.at[0], recv_sem=bulk_r.at[0],
            device_id={"band": t}, device_id_type=MESH,
        ).start()
        return carry

    lax.fori_loop(1, 128, push_density, 0)
    rn[band] = sn[band]

    for q in range(4):
        twins[q].wait_recv()

        def add_twin(i, carry):
            x_lo_, zz, yy = i // 32, lax.rem(i // 4, 8), lax.rem(i, 4)
            v = part[i, c] + twin[i]
            for x_hi in range(2):
                pos = x_hi * 2 + x_lo_
                qa[pos, yy * 8 + zz] = v[x_hi * 16 : x_hi * 16 + 8]
                qb[yy, pos * 8 + zz] = v[x_hi * 16 + 8 : x_hi * 16 + 16]
            return carry

        lax.fori_loop(q * 16, q * 16 + 16, add_twin, 0)
    first_a = [send(qa.at[p], ra.at[d], 4 + d, at(x_=p)) for d, p in enumerate(x_peers)]
    first_b = [send(qb.at[p], rb.at[d], 7 + d, at(y_=p)) for d, p in enumerate(y_peers)]

    me = s * 128 + band

    def push_spectrum(d, carry):
        t = lax.rem(me + d, 256)
        pltpu.make_async_remote_copy(
            src_ref=sp.at[t], dst_ref=rsp.at[me], send_sem=bulk_s.at[1], recv_sem=bulk_r.at[1],
            device_id={"band": lax.rem(t, 128), "spin": t // 128}, device_id_type=MESH,
        ).start()
        return carry

    lax.fori_loop(1, 256, push_spectrum, 0)
    rsp[me] = sp[me]

    load_dz.wait()
    all_n = rn.at[pl.ds(0, 127)]
    pltpu.make_async_copy(all_n, all_n, bulk_r.at[0]).wait()
    gz.reshape(256, 128)[...] = product(pair(dz), split(rn.reshape(256, 128)[...]))

    def push_back(d, carry):
        t = lax.rem(band + d, 128)
        pltpu.make_async_remote_copy(
            src_ref=gz.at[t], dst_ref=rg.at[band], send_sem=bulk_s.at[2], recv_sem=bulk_r.at[2],
            device_id={"band": t}, device_id_type=MESH,
        ).start()
        return carry

    lax.fori_loop(1, 128, push_back, 0)
    rg[band] = gz[band]

    for copy in first_a:
        copy.wait_recv()
    for t in range(4):
        sub = pl.ds(t * 8, 8)
        a1[t] = (qa[x, sub] + ra[0, sub]) + (ra[1, sub] + ra[2, sub])
    second_a = [send(a1.at[p], ra2.at[d], 10 + d, at(y_=p)) for d, p in enumerate(y_peers)]
    for copy in first_b:
        copy.wait_recv()
    for t in range(4):
        sub = pl.ds(t * 8, 8)
        b1[t] = (qb[y, sub] + rb[0, sub]) + (rb[1, sub] + rb[2, sub])
    second_b = [send(b1.at[p], rb2.at[d], 13 + d, at(x_=p)) for d, p in enumerate(x_peers)]

    load_factor.wait()
    load_tz.wait()
    lane = lax.broadcasted_iota(jnp.int32, (256, 128), 1)
    row = lax.broadcasted_iota(jnp.int32, (256, 128), 0)
    low = lane < 64
    unit_x, unit_y, unit_z = 2.0 * np.pi / NX, 2.0 * np.pi / NY, 2.0 * np.pi / NZ
    ky = jnp.where(low, lane, lane - 64) - 64 * s
    fy = unit_y * ky.astype(F32)
    fz = unit_z * jnp.where(row >= NZ // 2, row - NZ, row).astype(F32)
    fx = unit_x * jnp.full((1, 128), jnp.where(band >= NX // 2, band - NX, band).astype(F32))
    length_sq = fx * fx + fy * fy + fz * fz
    positive = length_sq > 0
    inverse = jnp.where(positive, 1.0 / jnp.where(positive, length_sq, 1.0), 0.0)
    f0, f1 = factor[0], factor[1]
    first = jnp.where(s == 0, f0, pltpu.roll(f0, 64, 1))
    second = jnp.where(s == 0, pltpu.roll(f1, 64, 1), f1)
    local = 2.0 * jnp.where(low, first, second)

    all_sp = rsp.at[pl.ds(0, 255)]
    pltpu.make_async_copy(all_sp, all_sp, bulk_r.at[1]).wait()
    rsp_flat = rsp.reshape(512, 128)
    planes = (rsp_flat[0:256] + rsp_flat[256:512]) * (1.0 / CELLS)
    crossed = pltpu.roll(planes, 64, 1)
    crossed = jnp.where(low, crossed, -crossed)
    spectrum = product(pair(tz), split(jnp.concatenate([planes, crossed], axis=0)))
    hartree = (4.0 * np.pi) * (spectrum * spectrum) * inverse
    weighting = 2.0 * hartree * inverse + spectrum * local

    def down(value):
        return jnp.sum(value, axis=0, keepdims=True)

    sum_h = down(hartree)
    sum_1, sum_z, sum_zz = down(weighting), down(weighting * fz), down(weighting * fz * fz)
    fy1 = fy[0:1]
    spectral = [
        fx * fx * sum_1 - sum_h, fy1 * fy1 * sum_1 - sum_h, sum_zz - sum_h, fy1 * sum_z, fx * sum_z, fx * fy1 * sum_1
    ]

    for copy in second_a:
        copy.wait_recv()
    ab[:, 0] = (a1[y] + ra2[0]) + (ra2[1] + ra2[2])
    for copy in second_b:
        copy.wait_recv()
    ab[:, 1] = (b1[x] + rb2[0]) + (rb2[1] + rb2[2])
    last = [send(ab.at[p], rz.at[d], 16 + d, at(z_=p)) for d, p in enumerate(z_peers)]

    pltpu.make_async_copy(all_n, rg.at[pl.ds(0, 127)], bulk_r.at[2]).wait()
    rg_flat = rg.reshape(256, 128)
    xc = [jnp.zeros((1, 128), F32)] * 6
    pairs = ((0, 0), (1, 1), (2, 2), (1, 2), (0, 2), (0, 1))
    for zz in range(2):
        n = dens[zz]
        grads = (gradx[zz], grady[zz], rg_flat[pl.ds(zz, 128, stride=2), :])
        square = grads[0] * grads[0] + grads[1] * grads[1] + grads[2] * grads[2]
        square_out[zz] = square
        room = 4.0 * n * n + 1.0
        kernel = jnp.exp(jnp.log(n) * (-1.0 / 3.0)) * room / (room + square)
        scaled = [kernel * g for g in grads]
        xc = [t + down(scaled[a] * grads[b]) for t, (a, b) in zip(xc, pairs)]

    g = [spacing * (miller[a].astype(F32) + kpoint[a]) for a in range(3)]
    for copy in last:
        copy.wait_recv()
    weight = ab[z]
    for d in range(7):
        weight = weight + rz[d]
    weight = weight.reshape(16, 128)
    density_out[...] = 0.5 * (g[0] * g[0] + g[1] * g[1] + g[2] * g[2]) * weight
    kinetic = [down(weight * g[a] * g[b]) for a, b in pairs]
    lines = [spectral[a] - kinetic[a] * (1.0 / NPW) - xc[a] * (1.0 / CELLS) for a in range(6)]
    held[0] = jnp.concatenate(lines + [jnp.zeros((2, 128), F32)], axis=0)

    plane_me = (x * 4 + y) * 2 + c
    stages = ((tot_z, z, [at(z_=p) for p in z_peers], 8), (tot_p, plane_me, plane, 32))
    k = 0
    for stage, (slots, mine, peers, count) in enumerate(stages):
        copies = []
        for peer in peers:
            copy = pltpu.make_async_remote_copy(
                src_ref=held.at[stage], dst_ref=slots.at[mine], send_sem=tsem_s.at[k], recv_sem=tsem_r.at[k],
                device_id=peer, device_id_type=MESH,
            )
            copy.start()
            copies.append(copy)
            k += 1
        slots[mine] = held[stage]
        for copy in copies:
            copy.wait_recv()
        pending += copies
        level = [slots[j] for j in range(count)]
        while len(level) > 1:
            level = [level[j] + level[j + 1] for j in range(0, len(level), 2)]
        if stage == 0:
            held[1] = level[0]
    for a in range(6):
        stress[a] = jnp.sum(level[0][a : a + 1, :])

    for copy in pending:
        copy.wait_send()
    for k, ref in ((0, all_n), (1, all_sp), (2, all_n)):
        pltpu.make_async_copy(ref, ref, bulk_s.at[k]).wait()


def shards(coefficients, occupation, miller, density, local_factor):
    pairs = coefficients[0].reshape(2, 2, NPW // 128, 128).transpose(0, 2, 1, 3).reshape(2, NPW // 64, 128)
    ty, tx, tz, dx, dz = [jnp.asarray(t) for t in tables()]
    vmem, smem, far = (pl.BlockSpec(memory_space=m) for m in (pltpu.VMEM, pltpu.SMEM, pltpu.HBM))
    held = [(pairs.shape, BF16), ((2, 128, 128), F32), ((2, 256, 128), F32)] + [(t.shape, BF16) for t in (ty, tx, tz, dx, dz)]
    scratch = held + [
        (shape, F32)
        for shape in (
            (128, 2, 128), (128, 2, 128), (128, 2, 128), (128, 2, 128), (256, 2, 128), (256, 2, 128),
            (64, 2, 32, 128), (64, 32, 128), (4, 32, 8, 128), (4, 32, 8, 128), (3, 32, 8, 128), (3, 32, 8, 128),
            (4, 8, 8, 128), (4, 8, 8, 128), (3, 8, 8, 128), (3, 8, 8, 128), (8, 2, 8, 128), (7, 2, 8, 128), (128, 128),
            (2, 8, 128), (8, 8, 128), (32, 8, 128),
            (2, 128, 128), (2, 128, 128),
        )
    ]
    dma = pltpu.SemaphoreType.DMA
    stress, kinetic_density, square = pl.pallas_call(
        stress_kernel,
        out_shape=(
            jax.ShapeDtypeStruct((6,), F32),
            jax.ShapeDtypeStruct((16, 128), F32),
            jax.ShapeDtypeStruct((2, 128, 128), F32),
        ),
        in_specs=[smem, vmem] + [far] * 8,
        out_specs=(smem, vmem, vmem),
        scratch_shapes=[pltpu.VMEM(*one) for one in scratch]
        + [pltpu.SemaphoreType.REGULAR, dma((8,)), dma((23,)), dma((23,)), dma((3,)), dma((3,)), dma((38,)), dma((38,))],
        compiler_params=pltpu.CompilerParams(collective_id=0, has_side_effects=True),
    )(
        occupation, miller.reshape(3, 16, 128), pairs, density[0], local_factor.reshape(2, 256, 128), ty, tx, tz, dx, dz
    )
    return (stress, kinetic_density.reshape(-1), square[None])


def solution(mesh):
    return jax.shard_map(
        shards,
        mesh=mesh,
        in_specs=(
            P("spin", None, "band", None),
            P("spin", "band"),
            P(None, ("band", "spin")),
            P("spin", "band", None, None),
            P(None, None, "band", None),
        ),
        out_specs=(P(), P(("band", "spin")), P("spin", "band", None, None)),
        check_vma=False,
    )
```

time: 369 us -> 58.5 us (0.16)
  waiting for transfers between devices: 219 us -> 0 us
  Pallas kernels: 0 us -> 52.2 us
  blocking collectives: 40 us -> 0 us
  matrix products: 31.6 us -> 0 us
  starting transfers between devices: 31.3 us -> 0 us
  between operations: 16 us -> 0.64 us
  local copies, waits for them, and re-layouts: 19.6 us -> 5.4 us
  other arithmetic: 11.1 us -> 0 us
    unnamed x2 -> x0, waiting for transfers between devices: 203 us -> none
    pallas_call x0 -> x1, Pallas kernels: none -> 52.2 us  [shards(): pl.pallas_call(stress_kernel, out_shape=(jax.ShapeDtypeStruct((6,), F32),...]
    psum x5 -> x0, blocking collectives: 40 us -> none  [by_axis(): shard = lax.psum(shard, axis)]
    dot_general x14 -> x0, matrix products: 31.6 us -> none  [the longest x1 17 us: shards(): jnp.dot(weights[0], squares, precision=highest)]
    all_to_all x3 -> x0, starting transfers between devices: 31.1 us -> none  [the longest x1 14.9 us: sent_together(): lax.all_to_all(both, axis, split_axis=split_dim, concat_axis=concat_dim,...]
    all_to_all x3 -> x0, waiting for transfers between devices: 15.5 us -> none  [the longest x1 12.4 us: shards(): lax.all_to_all(gradz_col, BAND, split_axis=1, concat_axis=2, tiled=True)]
    another operation x4 -> x0, local copies, waits for them, and re-layouts: 15.1 us -> none  [six_sums(): jnp.stack([jnp.sum(weighting * first_axis * first_axis), jnp.sum(weightin...]
    reduce_sum x5 -> x0, other arithmetic: 5.56 us -> none  [the longest x2 2.73 us: six_sums(): jnp.sum(weighting * first_axis * second_axis)]
  transfers between devices with their start and end apart: 4 -> 0, of which waited for: 3 -> 0; matrix products, arithmetic and copies ran while one was open for 13% -> 0% of each run, Pallas kernels for 0% -> 0%
where the time goes in v3:
time: 58.5 us; the launch traced here: 58.2 us
  Pallas kernels  52.2 us (89%)
  local copies, waits for them, and re-layouts  5.4 us (9%)
  between operations  0.64 us (1%)
    pallas_call x1, Pallas kernels, shards(): pl.pallas_call(stress_kernel, out_shape=(jax.ShapeDtypeStruct((6,), F32),...  52.2 us
    unnamed x4, local copies, waits for them, and re-layouts  5.4 us

profile of v3, /device:TPU:1, one launch (start us, length us, event | category | flops | bytes accessed | tf_op | source)
XLA Modules:
  0.0 58.2 jit_solution(18097765026883986587)
XLA Ops:
  0.6 1.4 %copy.16 = s32[1,3,16,128]{3,2,1,0:T(8,128)} copy(s32[1,3,16,128]{3,1,2,0:T(4,128)} %bitcast.18) | data formatting | bytes 49152
  2.0 52.2 %shard_map.121 = (f32[6]{0:T(128)}, f32[16,128]{1,0:T(8,128)}, f32[2,128,128]{2,1,0:T(8,128)}) custom-call(s32[1,2]{1,0:T(1,128)} %occ.1, s32[3,16,128]{2,1,0:T(8,128)} %bitcast.17, bf16[2,8192,128]{2,1,0:T(8,128)(2,1)} %bitcast.13, f32[2,128,128]{2,1,0:T(8,128)} %bitcast.15, f32[2,256,128]{2,1,0:T(8,128)} %bitcast.14, ...), custom_call_target="tpu_custom_call" | custom-call | tf_op jit(solution)/shard_map/pallas_call | solution.py:356
  54.2 1.2 %copy.20 = f32[6]{0:T(128)} copy(f32[6]{0:T(128)} %get-tuple-element.12) | data formatting | bytes 48
  55.4 1.3 %copy.21 = f32[2048]{0:T(1024)} copy(f32[2048]{0:T(1024)} %bitcast.19) | data formatting | bytes 16384
  56.7 1.6 %copy.22 = f32[1,2,128,128]{3,2,1,0:T(8,128)} copy(f32[1,2,128,128]{3,2,1,0:T(8,128)} %bitcast.16) | data formatting | bytes 262144

commit v4 on v3

--- a/solution.py
+++ b/solution.py
@@ -11,6 +11,7 @@
 NY = 128
 NZ = 256
 CELLS = NX * NY * NZ
+SPLIT = 96
 MESH = pl.DeviceIdType.MESH
 F32, BF16 = jnp.float32, jnp.bfloat16
 
@@ -69,13 +70,13 @@
 
 
 def stress_kernel(
-    occ, miller, coef_any, dens_any, factor_any, ty_any, tx_any, tz_any, dx_any, dz_any,
-    stress, density_out, square_out,
-    coef, dens, factor, ty, tx, tz, dx, dz,
+    occ_any, miller_any, coef_any, dens_any, factor_any, ty_any, tx_any, tz_any, dx_any, dz_any,
+    totals_out, density_out, square_out,
+    occ, miller, coef, dens, factor, ty, tx, tz, dx, dz,
     sn, rn, gz, rg, sp, rsp,
-    part, twin, qa, qb, ra, rb, a1, b1, ra2, rb2, ab, rz, tmp,
-    held, tot_z, tot_p,
-    gradx, grady, far, lsem, ssem, rsem, bulk_s, bulk_r, tsem_s, tsem_r,
+    part, twin, qa, qb, ra, rb, ha, hb, a1, b1, ra2, rb2, ab, rz, tmp,
+    held, tot_z, tot_p, density, square_held,
+    gradx, grady, far, lsem, osem, ssem, rsem, bulk_s, bulk_r, tsem_s, tsem_r,
 ):
     band, s = lax.axis_index("band"), lax.axis_index("spin")
     x_lo, z, y, c = band // 64, lax.rem(band // 8, 8), lax.rem(band // 2, 4), lax.rem(band, 2)
@@ -96,14 +97,22 @@
         at(x_=lax.rem(x + d // 8, 4), y_=lax.rem(y + d // 2, 4), c_=lax.rem(c + d, 2)) for d in range(1, 32)
     ]
 
-    locals_ = []
-    for k, (src, dst) in enumerate(
-        ((dens_any, dens), (ty_any, ty), (tx_any, tx), (dx_any, dx), (coef_any, coef), (dz_any, dz), (tz_any, tz), (factor_any, factor))
-    ):
+    def load(src, dst, k):
         copy = pltpu.make_async_copy(src, dst, lsem.at[k])
         copy.start()
-        locals_.append(copy)
-    load_dens, load_ty, load_tx, load_dx, load_coef, load_dz, load_tz, load_factor = locals_
+        return copy
+
+    load_occ = load(occ_any, occ, 0)
+    load_coef = [
+        load(coef_any.at[:, pl.ds(q * 2048, 2048)], coef.at[:, pl.ds(q * 2048, 2048)], 1 + q) for q in range(4)
+    ]
+    load_dens, load_ty, load_tx, load_dx, load_dz, load_tz, load_factor, load_miller = [
+        load(src, dst, 5 + k)
+        for k, (src, dst) in enumerate(
+            ((dens_any, dens), (ty_any, ty), (tx_any, tx), (dx_any, dx), (dz_any, dz), (tz_any, tz),
+             (factor_any, factor), (miller_any, miller))
+        )
+    ]
     barrier = pltpu.get_barrier_semaphore()
     for p in z_peers:
         pl.semaphore_signal(barrier, inc=1, device_id=at(z_=p), device_id_type=MESH)
@@ -120,32 +129,35 @@
         pending.append(copy)
         return copy
 
+    load_occ.wait()
+    w0 = jnp.full((64, 128), occ[0, 0].astype(F32)) / occupation_unit
+    w1 = jnp.full((64, 128), occ[0, 1].astype(F32)) / occupation_unit
+
+    def squares(i, carry):
+        for u in range(2):
+            rows = pl.ds(pl.multiple_of(i * 256 + u * 128, 128), 128)
+            re = coef[0, rows, :].astype(F32)
+            im = coef[1, rows, :].astype(F32)
+            tmp[u] = re * re + im * im
+            both = w0 * tmp[u, pl.ds(0, 64, stride=2), :] + w1 * tmp[u, pl.ds(1, 64, stride=2), :]
+            part[i * 2 + u] = both.reshape(2, 32, 128)
+        return carry
+
+    for q in range(4):
+        load_coef[q].wait()
+        lax.fori_loop(q * 8, q * 8 + 8, squares, 0)
+
+    pl.semaphore_wait(barrier, 38)
+    twins = [
+        send(part.at[pl.ds(q * 16, 16), other], twin.at[pl.ds(q * 16, 16)], q, at(c_=other)) for q in range(4)
+    ]
+    for p in z_peers:
+        pl.semaphore_signal(far, inc=1, device_id=at(z_=p), device_id_type=MESH)
+
     load_dens.wait()
     sn_flat = sn.reshape(256, 128)
     for zz in range(2):
         sn_flat[pl.ds(zz, 128, stride=2), :] = dens[zz]
-
-    load_coef.wait()
-    w0 = jnp.full((64, 128), occ[0, 0].astype(F32)) / occupation_unit
-    w1 = jnp.full((64, 128), occ[0, 1].astype(F32)) / occupation_unit
-
-    def squares(i, carry):
-        rows = pl.ds(pl.multiple_of(i * 128, 128), 128)
-        re = coef[0, rows, :].astype(F32)
-        im = coef[1, rows, :].astype(F32)
-        tmp[...] = re * re + im * im
-        both = w0 * tmp[pl.ds(0, 64, stride=2), :] + w1 * tmp[pl.ds(1, 64, stride=2), :]
-        part[i] = both.reshape(2, 32, 128)
-        return carry
-
-    lax.fori_loop(0, 64, squares, 0)
-
-    pl.semaphore_wait(barrier, 38)
-    for p in z_peers:
-        pl.semaphore_signal(far, inc=1, device_id=at(z_=p), device_id_type=MESH)
-    twins = [
-        send(part.at[pl.ds(q * 16, 16), other], twin.at[pl.ds(q * 16, 16)], q, at(c_=other)) for q in range(4)
-    ]
 
     load_ty.wait()
     load_tx.wait()
@@ -163,6 +175,42 @@
         for half in range(2):
             sp_flat[pl.ds(half * 256 + zz, 128, stride=2), :] = turned[:, half * 128 : half * 128 + 128]
 
+    for q in range(4):
+        twins[q].wait_recv()
+
+        def add_twin(j, carry):
+            for u in range(4):
+                i = j * 4 + u
+                x_lo_, zz, yy = i // 32, lax.rem(i // 4, 8), u
+                v = part[i, c] + twin[i]
+                for x_hi in range(2):
+                    pos = x_hi * 2 + x_lo_
+                    qa[pos, yy * 8 + zz] = v[x_hi * 16 : x_hi * 16 + 8]
+                    qb[yy, pos * 8 + zz] = v[x_hi * 16 + 8 : x_hi * 16 + 16]
+            return carry
+
+        lax.fori_loop(q * 4, q * 4 + 4, add_twin, 0)
+    top, low_half = pl.ds(0, 16), pl.ds(16, 16)
+    rings = (
+        (qa, ra, ha, x_peers, lambda p: at(x_=p), 4),
+        (qb, rb, hb, y_peers, lambda p: at(y_=p), 10),
+    )
+    relays, firsts = [], []
+    for own, got, half, (right, across, left), where, k in rings:
+        relays.append(
+            (
+                send(own.at[across, top], half.at[0], k, where(right)),
+                send(own.at[across, low_half], half.at[1], k + 1, where(left)),
+            )
+        )
+    for own, got, half, (right, across, left), where, k in rings:
+        firsts.append(
+            [
+                send(own.at[right, low_half], got.at[0, low_half], k + 2, where(right)),
+                send(own.at[left, top], got.at[1, top], k + 3, where(left)),
+            ]
+        )
+
     pl.semaphore_wait(far, 7)
 
     def push_density(d, carry):
@@ -176,22 +224,6 @@
     lax.fori_loop(1, 128, push_density, 0)
     rn[band] = sn[band]
 
-    for q in range(4):
-        twins[q].wait_recv()
-
-        def add_twin(i, carry):
-            x_lo_, zz, yy = i // 32, lax.rem(i // 4, 8), lax.rem(i, 4)
-            v = part[i, c] + twin[i]
-            for x_hi in range(2):
-                pos = x_hi * 2 + x_lo_
-                qa[pos, yy * 8 + zz] = v[x_hi * 16 : x_hi * 16 + 8]
-                qb[yy, pos * 8 + zz] = v[x_hi * 16 + 8 : x_hi * 16 + 16]
-            return carry
-
-        lax.fori_loop(q * 16, q * 16 + 16, add_twin, 0)
-    first_a = [send(qa.at[p], ra.at[d], 4 + d, at(x_=p)) for d, p in enumerate(x_peers)]
-    first_b = [send(qb.at[p], rb.at[d], 7 + d, at(y_=p)) for d, p in enumerate(y_peers)]
-
     me = s * 128 + band
 
     def push_spectrum(d, carry):
@@ -202,7 +234,15 @@
         ).start()
         return carry
 
-    lax.fori_loop(1, 256, push_spectrum, 0)
+    lax.fori_loop(1, SPLIT, push_spectrum, 0)
+    for (own, got, half, (right, across, left), where, k), (to_right, to_left), first in zip(rings, relays, firsts):
+        to_right.wait_recv()
+        half[2] = own[right, top] + half[0]
+        first.append(send(half.at[2], got.at[0, top], k + 4, where(right)))
+        to_left.wait_recv()
+        half[3] = own[left, low_half] + half[1]
+        first.append(send(half.at[3], got.at[1, low_half], k + 5, where(left)))
+    lax.fori_loop(SPLIT, 256, push_spectrum, 0)
     rsp[me] = sp[me]
 
     load_dz.wait()
@@ -221,18 +261,18 @@
     lax.fori_loop(1, 128, push_back, 0)
     rg[band] = gz[band]
 
-    for copy in first_a:
+    for copy in firsts[0]:
         copy.wait_recv()
     for t in range(4):
         sub = pl.ds(t * 8, 8)
-        a1[t] = (qa[x, sub] + ra[0, sub]) + (ra[1, sub] + ra[2, sub])
-    second_a = [send(a1.at[p], ra2.at[d], 10 + d, at(y_=p)) for d, p in enumerate(y_peers)]
-    for copy in first_b:
+        a1[t] = qa[x, sub] + (ra[0, sub] + ra[1, sub])
+    second_a = [send(a1.at[p], ra2.at[d], 16 + d, at(y_=p)) for d, p in enumerate(y_peers)]
+    for copy in firsts[1]:
         copy.wait_recv()
     for t in range(4):
         sub = pl.ds(t * 8, 8)
-        b1[t] = (qb[y, sub] + rb[0, sub]) + (rb[1, sub] + rb[2, sub])
-    second_b = [send(b1.at[p], rb2.at[d], 13 + d, at(x_=p)) for d, p in enumerate(x_peers)]
+        b1[t] = qb[y, sub] + (rb[0, sub] + rb[1, sub])
+    second_b = [send(b1.at[p], rb2.at[d], 19 + d, at(x_=p)) for d, p in enumerate(x_peers)]
 
     load_factor.wait()
     load_tz.wait()
@@ -278,7 +318,7 @@
     for copy in second_b:
         copy.wait_recv()
     ab[:, 1] = (b1[x] + rb2[0]) + (rb2[1] + rb2[2])
-    last = [send(ab.at[p], rz.at[d], 16 + d, at(z_=p)) for d, p in enumerate(z_peers)]
+    last = [send(ab.at[p], rz.at[d], 22 + d, at(z_=p)) for d, p in enumerate(z_peers)]
 
     pltpu.make_async_copy(all_n, rg.at[pl.ds(0, 127)], bulk_r.at[2]).wait()
     rg_flat = rg.reshape(256, 128)
@@ -288,23 +328,28 @@
         n = dens[zz]
         grads = (gradx[zz], grady[zz], rg_flat[pl.ds(zz, 128, stride=2), :])
         square = grads[0] * grads[0] + grads[1] * grads[1] + grads[2] * grads[2]
-        square_out[zz] = square
+        square_held[zz] = square
         room = 4.0 * n * n + 1.0
         kernel = jnp.exp(jnp.log(n) * (-1.0 / 3.0)) * room / (room + square)
         scaled = [kernel * g for g in grads]
         xc = [t + down(scaled[a] * grads[b]) for t, (a, b) in zip(xc, pairs)]
 
-    g = [spacing * (miller[a].astype(F32) + kpoint[a]) for a in range(3)]
+    store_square = pltpu.make_async_copy(square_held, square_out, osem.at[0])
+    store_square.start()
+    load_miller.wait()
+    g = [spacing * (miller[:, a].astype(F32) + kpoint[a]) for a in range(3)]
     for copy in last:
         copy.wait_recv()
     weight = ab[z]
     for d in range(7):
         weight = weight + rz[d]
     weight = weight.reshape(16, 128)
-    density_out[...] = 0.5 * (g[0] * g[0] + g[1] * g[1] + g[2] * g[2]) * weight
+    density[...] = 0.5 * (g[0] * g[0] + g[1] * g[1] + g[2] * g[2]) * weight
     kinetic = [down(weight * g[a] * g[b]) for a, b in pairs]
     lines = [spectral[a] - kinetic[a] * (1.0 / NPW) - xc[a] * (1.0 / CELLS) for a in range(6)]
-    held[0] = jnp.concatenate(lines + [jnp.zeros((2, 128), F32)], axis=0)
+    sums = jnp.sum(jnp.concatenate(lines + [jnp.zeros((2, 128), F32)], axis=0), axis=1, keepdims=True)
+    diagonal = lax.broadcasted_iota(jnp.int32, (8, 128), 0) == lax.broadcasted_iota(jnp.int32, (8, 128), 1)
+    held[0] = down(jnp.where(diagonal, sums, 0.0))
 
     plane_me = (x * 4 + y) * 2 + c
     stages = ((tot_z, z, [at(z_=p) for p in z_peers], 8), (tot_p, plane_me, plane, 32))
@@ -320,54 +365,95 @@
             copies.append(copy)
             k += 1
         slots[mine] = held[stage]
+        if stage == 0:
+            store_density = pltpu.make_async_copy(density, density_out, osem.at[1])
+            store_density.start()
         for copy in copies:
             copy.wait_recv()
         pending += copies
-        level = [slots[j] for j in range(count)]
-        while len(level) > 1:
-            level = [level[j] + level[j + 1] for j in range(0, len(level), 2)]
-        if stage == 0:
-            held[1] = level[0]
-    for a in range(6):
-        stress[a] = jnp.sum(level[0][a : a + 1, :])
+        held[stage + 1] = down(slots.reshape(count, 128)[...])
+    store_totals = pltpu.make_async_copy(held.at[2], totals_out, osem.at[2])
+    store_totals.start()
 
     for copy in pending:
         copy.wait_send()
     for k, ref in ((0, all_n), (1, all_sp), (2, all_n)):
         pltpu.make_async_copy(ref, ref, bulk_s.at[k]).wait()
+    store_square.wait()
+    store_density.wait()
+    store_totals.wait()
+
+
+def emit_kernel(totals_any, density_any, square_any, stress_out, density_out, square_out, totals, stress, density, square, sem):
+    into = [
+        pltpu.make_async_copy(src, dst, sem.at[k])
+        for k, (src, dst) in enumerate(((square_any, square), (density_any, density), (totals_any, totals)))
+    ]
+    for copy in into:
+        copy.start()
+    out = [
+        pltpu.make_async_copy(src, dst, sem.at[3 + k])
+        for k, (src, dst) in enumerate(((square, square_out), (density, density_out), (stress, stress_out)))
+    ]
+    for k in range(2):
+        into[k].wait()
+        out[k].start()
+    into[2].wait()
+    for a in range(6):
+        stress[a] = totals[0, a]
+    out[2].start()
+    for copy in out:
+        copy.wait()
 
 
 def shards(coefficients, occupation, miller, density, local_factor):
     pairs = coefficients[0].reshape(2, 2, NPW // 128, 128).transpose(0, 2, 1, 3).reshape(2, NPW // 64, 128)
     ty, tx, tz, dx, dz = [jnp.asarray(t) for t in tables()]
-    vmem, smem, far = (pl.BlockSpec(memory_space=m) for m in (pltpu.VMEM, pltpu.SMEM, pltpu.HBM))
-    held = [(pairs.shape, BF16), ((2, 128, 128), F32), ((2, 256, 128), F32)] + [(t.shape, BF16) for t in (ty, tx, tz, dx, dz)]
-    scratch = held + [
+    hbm = pl.BlockSpec(memory_space=pltpu.HBM)
+    millers = miller.reshape(3, 16, 128).transpose(1, 0, 2)
+    loaded = [(millers.shape, jnp.int32), (pairs.shape, BF16), ((2, 128, 128), F32), ((2, 256, 128), F32)]
+    loaded += [(t.shape, BF16) for t in (ty, tx, tz, dx, dz)]
+    scratch = loaded + [
         (shape, F32)
         for shape in (
             (128, 2, 128), (128, 2, 128), (128, 2, 128), (128, 2, 128), (256, 2, 128), (256, 2, 128),
-            (64, 2, 32, 128), (64, 32, 128), (4, 32, 8, 128), (4, 32, 8, 128), (3, 32, 8, 128), (3, 32, 8, 128),
-            (4, 8, 8, 128), (4, 8, 8, 128), (3, 8, 8, 128), (3, 8, 8, 128), (8, 2, 8, 128), (7, 2, 8, 128), (128, 128),
-            (2, 8, 128), (8, 8, 128), (32, 8, 128),
+            (64, 2, 32, 128), (64, 32, 128), (4, 32, 8, 128), (4, 32, 8, 128), (2, 32, 8, 128), (2, 32, 8, 128),
+            (4, 16, 8, 128), (4, 16, 8, 128),
+            (4, 8, 8, 128), (4, 8, 8, 128), (3, 8, 8, 128), (3, 8, 8, 128), (8, 2, 8, 128), (7, 2, 8, 128), (2, 128, 128),
+            (3, 1, 128), (8, 1, 128), (32, 1, 128), (16, 128), (2, 128, 128),
             (2, 128, 128), (2, 128, 128),
         )
     ]
     dma = pltpu.SemaphoreType.DMA
+    results = (
+        jax.ShapeDtypeStruct((1, 128), F32),
+        jax.ShapeDtypeStruct((16, 128), F32),
+        jax.ShapeDtypeStruct((2, 128, 128), F32),
+    )
+    totals, kinetic_density, square = pl.pallas_call(
+        stress_kernel,
+        out_shape=results,
+        in_specs=[hbm] * 10,
+        out_specs=(hbm,) * 3,
+        scratch_shapes=[pltpu.SMEM((1, 2), jnp.int32)]
+        + [pltpu.VMEM(*one) for one in scratch]
+        + [pltpu.SemaphoreType.REGULAR, dma((13,)), dma((3,)), dma((29,)), dma((29,)), dma((3,)), dma((3,))]
+        + [dma((38,)), dma((38,))],
+        compiler_params=pltpu.CompilerParams(collective_id=0, has_side_effects=True),
+    )(occupation, millers, pairs, density[0], local_factor.reshape(2, 256, 128), ty, tx, tz, dx, dz)
     stress, kinetic_density, square = pl.pallas_call(
-        stress_kernel,
-        out_shape=(
-            jax.ShapeDtypeStruct((6,), F32),
-            jax.ShapeDtypeStruct((16, 128), F32),
-            jax.ShapeDtypeStruct((2, 128, 128), F32),
-        ),
-        in_specs=[smem, vmem] + [far] * 8,
-        out_specs=(smem, vmem, vmem),
-        scratch_shapes=[pltpu.VMEM(*one) for one in scratch]
-        + [pltpu.SemaphoreType.REGULAR, dma((8,)), dma((23,)), dma((23,)), dma((3,)), dma((3,)), dma((38,)), dma((38,))],
-        compiler_params=pltpu.CompilerParams(collective_id=0, has_side_effects=True),
-    )(
-        occupation, miller.reshape(3, 16, 128), pairs, density[0], local_factor.reshape(2, 256, 128), ty, tx, tz, dx, dz
-    )
+        emit_kernel,
+        out_shape=(jax.ShapeDtypeStruct((6,), F32),) + results[1:],
+        in_specs=[hbm] * 3,
+        out_specs=(hbm,) * 3,
+        scratch_shapes=[
+            pltpu.SMEM((1, 128), F32),
+            pltpu.SMEM((6,), F32),
+            pltpu.VMEM((16, 128), F32),
+            pltpu.VMEM((2, 128, 128), F32),
+            dma((6,)),
+        ],
+    )(totals, kinetic_density, square)
     return (stress, kinetic_density.reshape(-1), square[None])
 
 

time: 58.5 us -> 47.6 us (0.81)
  local copies, waits for them, and re-layouts: 5.4 us -> 0 us
  Pallas kernels: 52.2 us -> 46.9 us
    unnamed x4 -> x0, local copies, waits for them, and re-layouts: 5.4 us -> none
    pallas_call x1 -> x2, Pallas kernels: 52.2 us -> 46.9 us  [the longest x1 45.2 us: shards(): pl.pallas_call(stress_kernel, out_shape=results, in_specs=[hbm] * 10, out...]
where the time goes in v4:
time: 47.6 us; the launch traced here: 47.5 us
  Pallas kernels  46.9 us (99%)
  between operations  0.64 us (1%)
    pallas_call x1, Pallas kernels, shards(): pl.pallas_call(stress_kernel, out_shape=results, in_specs=[hbm] * 10, out...  45.2 us
    pallas_call x1, Pallas kernels, shards(): pl.pallas_call(emit_kernel, out_shape=(jax.ShapeDtypeStruct((6,), F32),)...  1.62 us

profile of v4, /device:TPU:1, one launch (start us, length us, event | category | flops | bytes accessed | tf_op | source)
XLA Modules:
  0.0 47.5 jit_solution(8317489427032232265)
XLA Ops:
  0.6 45.2 %shard_map.121 = (f32[1,128]{1,0:T(1,128)}, f32[16,128]{1,0:T(8,128)}, f32[2,128,128]{2,1,0:T(8,128)}) custom-call(s32[1,2]{1,0:T(1,128)} %occ_any.1, s32[16,3,128]{2,1,0:T(4,128)} %bitcast.15, bf16[2,8192,128]{2,1,0:T(8,128)(2,1)} %bitcast.12, f32[2,128,128]{2,1,0:T(8,128)} %bitcast.14, f32[2,256,128]{2,1,0:T(8,128)} %bitcast.13, ...), custom_call_target="tpu_custom_call" | custom-call | tf_op jit(solution)/shard_map/pallas_call | solution.py:433
  45.9 1.6 %shard_map.122 = (f32[6]{0:T(128)}, f32[16,128]{1,0:T(8,128)}, f32[2,128,128]{2,1,0:T(8,128)}) custom-call(f32[1,128]{1,0:T(1,128)} %get-tuple-element.9.totals_any, f32[16,128]{1,0:T(8,128)} %get-tuple-element.10.density_any, f32[2,128,128]{2,1,0:T(8,128)} %get-tuple-element.11.square_any), custom_call_target="tpu_custom_call" | custom-call | tf_op jit(solution)/shard_map/pallas_call | solution.py:444

commit v5 on v4

v5 whole, which is shorter than its diff:
```python
import functools

import jax
import jax.numpy as jnp
import numpy as np
from jax import lax
from jax.experimental import pallas as pl
from jax.experimental.pallas import tpu as pltpu
from jax.sharding import PartitionSpec as P

NPW = 524288
NX = 128
NY = 128
NZ = 256
CELLS = NX * NY * NZ
MESH = pl.DeviceIdType.MESH
F32, BF16 = jnp.float32, jnp.bfloat16

occupation_unit = 1000.0
kpoint = (0.25, 0.125, 0.375)
spacing = 0.25


def derivative_table(length):
    apart = np.arange(length)[:, None] - np.arange(length)[None, :]
    angles = np.pi / length * np.where(apart == 0, 1, apart)
    return np.where(apart == 0, 0.0, 0.5 * (1.0 - 2.0 * (apart % 2)) * np.cos(angles) / np.sin(angles))


def fourier_tables(length):
    index = np.arange(length)
    phases = (index[:, None] * index[None, :]) % length * (2.0 * np.pi / length)
    return np.cos(phases), np.sin(phases)


def halves(table):
    table = np.asarray(table, np.float32)
    high = table.astype(BF16)
    return np.stack([high, (table - high.astype(np.float32)).astype(BF16)])


def tables():
    cos_y, sin_y = fourier_tables(NY)
    cos_x, sin_x = fourier_tables(NX)
    cos_z, sin_z = fourier_tables(NZ)
    lo, hi = slice(0, 64), slice(64, 128)
    re, im = cos_y, -sin_y
    along_y = np.concatenate(
        [re[:, lo], im[:, lo], re[:, hi], im[:, hi], im[:, lo], -re[:, lo], im[:, hi], -re[:, hi], derivative_table(NY).T],
        axis=1,
    )
    along_x = np.concatenate([cos_x, sin_x], axis=1)
    along_z = np.concatenate([cos_z, sin_z], axis=1)
    plane = np.concatenate([along_y, along_x, derivative_table(NX)], axis=1)
    column = np.concatenate([along_z, derivative_table(NZ)], axis=1)
    return [halves(t) for t in (plane, column)]


def split(value):
    high = value.astype(BF16)
    return high, (value - high.astype(F32)).astype(BF16)


def product(left, right):
    def dot(a, b):
        return jnp.dot(a, b, preferred_element_type=F32)

    return dot(left[0], right[0]) + (dot(left[0], right[1]) + dot(left[1], right[0]))


def pair(table, first, last):
    return table[0, :, first:last], table[1, :, first:last]


def stress_kernel(
    occ_any, miller_any, coef_any, dens_any, factor_any, plane_any, column_any,
    totals_out, density_out, square_out,
    occ, millers, coef, dens, far_plane, factor, in_plane, in_column,
    sn, rn, gz, rg, sp, rsp,
    part, twin, qa, qb, ra, rb, ha, hb, a1, b1, ra2, rb2, ab, rz, tmp,
    held, tot_z, tot_p, density, square_held,
    gradx, grady, far, lsem, osem, ssem, rsem, bulk_s, bulk_r,
):
    band, s = lax.axis_index("band"), lax.axis_index("spin")
    x_lo, z, y, c = band // 64, lax.rem(band // 8, 8), lax.rem(band // 2, 4), lax.rem(band, 2)
    x = s * 2 + x_lo
    other = 1 - c

    def at(x_=None, z_=None, y_=None, c_=None):
        x_ = x if x_ is None else x_
        z_ = z if z_ is None else z_
        y_ = y if y_ is None else y_
        c_ = c if c_ is None else c_
        return {"band": ((lax.rem(x_, 2) * 8 + z_) * 4 + y_) * 2 + c_, "spin": x_ // 2}

    x_peers = [lax.rem(x + d, 4) for d in (1, 2, 3)]
    y_peers = [lax.rem(y + d, 4) for d in (1, 2, 3)]
    z_peers = [lax.rem(z + d, 8) for d in range(1, 8)]
    plane = [
        at(x_=lax.rem(x + d // 8, 4), y_=lax.rem(y + d // 2, 4), c_=lax.rem(c + d, 2)) for d in range(1, 32)
    ]

    def load(src, dst, k):
        copy = pltpu.make_async_copy(src, dst, lsem.at[k])
        copy.start()
        return copy

    load_occ = load(occ_any, occ, 0)
    load_coef = [
        load(coef_any.at[:, pl.ds(q * 2048, 2048)], coef.at[:, pl.ds(q * 2048, 2048)], 1 + q) for q in range(4)
    ]
    barrier = pltpu.get_barrier_semaphore()
    for p in z_peers:
        pl.semaphore_signal(barrier, inc=1, device_id=at(z_=p), device_id_type=MESH)
    for peer in plane:
        pl.semaphore_signal(barrier, inc=1, device_id=peer, device_id_type=MESH)

    load_dens, load_plane, load_column, load_factor, load_miller = [
        load(src, dst, 5 + k)
        for k, (src, dst) in enumerate(
            ((dens_any, dens), (plane_any, in_plane), (column_any, in_column), (factor_any, factor),
             (miller_any, millers.at[z]))
        )
    ]
    def send(src, dst, k, peer):
        copy = pltpu.make_async_remote_copy(
            src_ref=src, dst_ref=dst, send_sem=ssem.at[0], recv_sem=rsem.at[k], device_id=peer, device_id_type=MESH
        )
        copy.start()
        return copy

    def arrived(ref, sem):
        pltpu.make_async_copy(ref, ref, sem).wait()

    load_occ.wait()
    w0 = jnp.full((64, 128), occ[0, 0].astype(F32)) / occupation_unit
    w1 = jnp.full((64, 128), occ[0, 1].astype(F32)) / occupation_unit

    def squares(i, carry):
        for u in range(2):
            rows = pl.ds(pl.multiple_of(i * 256 + u * 128, 128), 128)
            re = coef[0, rows, :].astype(F32)
            im = coef[1, rows, :].astype(F32)
            tmp[u] = re * re + im * im
            both = w0 * tmp[u, pl.ds(0, 64, stride=2), :] + w1 * tmp[u, pl.ds(1, 64, stride=2), :]
            part[i * 2 + u] = both.reshape(2, 32, 128)
        return carry

    for q in range(4):
        load_coef[q].wait()
        lax.fori_loop(q * 8, q * 8 + 8, squares, 0)

    pl.semaphore_wait(barrier, 38)
    twins = [
        send(part.at[pl.ds(q * 16, 16), other], twin.at[pl.ds(q * 16, 16)], q, at(c_=other)) for q in range(4)
    ]
    load_dens.wait()
    over_spin = send(dens.at[1 - s], far_plane, 4, at(x_=x_peers[1]))
    for p in z_peers:
        pl.semaphore_signal(far, inc=1, device_id=at(z_=p), device_id_type=MESH)
    load_miller.wait()
    for p in z_peers:
        send(millers.at[z], millers.at[z], 5, at(z_=p))

    sn_flat = sn.reshape(256, 128)
    for zz in range(2):
        sn_flat[pl.ds(zz, 128, stride=2), :] = dens[zz]

    load_plane.wait()
    from_y = product(split(dens[...].reshape(256, 128)), pair(in_plane, 512, 640))
    from_x = product(pair(in_plane, 896, 1024), split(jnp.concatenate([dens[0], dens[1]], axis=1)))
    for zz in range(2):
        grady[zz] = from_y[zz * 128 : zz * 128 + 128]
        gradx[zz] = from_x[:, zz * 128 : zz * 128 + 128]

    for q in range(4):
        twins[q].wait_recv()

        def add_twin(j, carry):
            for u in range(4):
                i = j * 4 + u
                x_lo_, zz, yy = i // 32, lax.rem(i // 4, 8), u
                v = part[i, c] + twin[i]
                for x_hi in range(2):
                    pos = x_hi * 2 + x_lo_
                    qa[pos, yy * 8 + zz] = v[x_hi * 16 : x_hi * 16 + 8]
                    qb[yy, pos * 8 + zz] = v[x_hi * 16 + 8 : x_hi * 16 + 16]
            return carry

        lax.fori_loop(q * 4, q * 4 + 4, add_twin, 0)
    top, low_half = pl.ds(0, 16), pl.ds(16, 16)
    rings = (
        (qa, ra, ha, x_peers, lambda p: at(x_=p), 6),
        (qb, rb, hb, y_peers, lambda p: at(y_=p), 9),
    )
    for own, got, half, (right, across, left), where, k in rings:
        send(own.at[across, top], half.at[0], k, where(right))
        send(own.at[across, low_half], half.at[1], k, where(left))
    pl.semaphore_wait(far, 7)

    def push_density(t, carry):
        pltpu.make_async_remote_copy(
            src_ref=sn.at[t], dst_ref=rn.at[band], send_sem=bulk_s.at[0], recv_sem=bulk_r.at[0],
            device_id={"band": t}, device_id_type=MESH,
        ).start()
        return carry

    lax.fori_loop(band + 1, 128, push_density, 0)
    lax.fori_loop(0, band, push_density, 0)
    rn[band] = sn[band]

    for own, got, half, (right, across, left), where, k in rings:
        send(own.at[right, low_half], got.at[0, low_half], k + 1, where(right))
        send(own.at[left, top], got.at[1, top], k + 1, where(left))

    over_spin.wait_recv()
    along = product(split(dens[s] + far_plane[...]), pair(in_plane, 0, 512))
    turned = product(pair(in_plane, 640, 896), split(jnp.concatenate([along[:, 0:256], along[:, 256:512]], axis=0)))
    sp_flat = sp.reshape(256, 128)
    for half in range(2):
        sp_flat[half * 128 : half * 128 + 128] = turned[:, half * 128 : half * 128 + 128]

    me = s * 128 + band

    def push_spectrum(to, t, carry):
        pltpu.make_async_remote_copy(
            src_ref=sp.at[to * 128 + t], dst_ref=rsp.at[band * 2 + s], send_sem=bulk_s.at[1], recv_sem=bulk_r.at[1],
            device_id={"band": t, "spin": to}, device_id_type=MESH,
        ).start()
        return carry

    for own, got, half, (right, across, left), where, k in rings:
        arrived(half.at[pl.ds(0, 2)], rsem.at[k])
        half[2] = own[right, top] + half[0]
        send(half.at[2], got.at[0, top], k + 1, where(right))
        half[3] = own[left, low_half] + half[1]
        send(half.at[3], got.at[1, low_half], k + 1, where(left))

    for to, start in ((1 - s, band), (s, band + 1)):
        push = functools.partial(push_spectrum, to)
        lax.fori_loop(start, 128, push, 0)
        lax.fori_loop(0, band, push, 0)
    rsp[band * 2 + s] = sp[me]

    arrived(ra, rsem.at[7])
    for t in range(4):
        sub = pl.ds(t * 8, 8)
        a1[t] = qa[x, sub] + (ra[0, sub] + ra[1, sub])
    for d, p in enumerate(y_peers):
        send(a1.at[p], ra2.at[d], 8, at(y_=p))
    arrived(rb, rsem.at[10])
    for t in range(4):
        sub = pl.ds(t * 8, 8)
        b1[t] = qb[y, sub] + (rb[0, sub] + rb[1, sub])
    for d, p in enumerate(x_peers):
        send(b1.at[p], rb2.at[d], 11, at(x_=p))

    load_column.wait()
    all_n = rn.at[pl.ds(0, 127)]
    arrived(all_n, bulk_r.at[0])
    gz.reshape(256, 128)[...] = product(pair(in_column, 512, 768), split(rn.reshape(256, 128)[...]))

    def push_back(t, carry):
        pltpu.make_async_remote_copy(
            src_ref=gz.at[t], dst_ref=rg.at[band], send_sem=bulk_s.at[2], recv_sem=bulk_r.at[2],
            device_id={"band": t}, device_id_type=MESH,
        ).start()
        return carry

    lax.fori_loop(band + 1, 128, push_back, 0)
    lax.fori_loop(0, band, push_back, 0)
    rg[band] = gz[band]

    load_factor.wait()
    lane = lax.broadcasted_iota(jnp.int32, (256, 128), 1)
    row = lax.broadcasted_iota(jnp.int32, (256, 128), 0)
    low = lane < 64
    unit_x, unit_y, unit_z = 2.0 * np.pi / NX, 2.0 * np.pi / NY, 2.0 * np.pi / NZ
    ky = jnp.where(low, lane, lane - 64) - 64 * s
    fy = unit_y * ky.astype(F32)
    fz = unit_z * jnp.where(row >= NZ // 2, row - NZ, row).astype(F32)
    fx = unit_x * jnp.full((1, 128), jnp.where(band >= NX // 2, band - NX, band).astype(F32))
    length_sq = fx * fx + fy * fy + fz * fz
    positive = length_sq > 0
    inverse = jnp.where(positive, 1.0 / jnp.where(positive, length_sq, 1.0), 0.0)
    f0, f1 = factor[0], factor[1]
    first = jnp.where(s == 0, f0, pltpu.roll(f0, 64, 1))
    second = jnp.where(s == 0, pltpu.roll(f1, 64, 1), f1)
    local = 2.0 * jnp.where(low, first, second)

    arrived(ra2, rsem.at[8])
    ab[:, 0] = (a1[y] + ra2[0]) + (ra2[1] + ra2[2])
    arrived(rb2, rsem.at[11])
    ab[:, 1] = (b1[x] + rb2[0]) + (rb2[1] + rb2[2])
    for d, p in enumerate(z_peers):
        send(ab.at[p], rz.at[d], 12, at(z_=p))

    def down(value):
        return jnp.sum(value, axis=0, keepdims=True)

    pairs = ((0, 0), (1, 1), (2, 2), (1, 2), (0, 2), (0, 1))
    arrived(millers.at[pl.ds(0, 7)], rsem.at[5])

    def wave(a, at_z):
        return spacing * (millers[at_z, :, a].astype(F32) + kpoint[a])

    kinetic = [jnp.zeros((1, 128), F32)] * 6
    for at_z in range(8):
        weight = ab[at_z].reshape(16, 128)
        g = [wave(a, at_z) for a in range(3)]
        scaled = [weight * one for one in g]
        kinetic = [t + down(scaled[a] * g[b]) for t, (a, b) in zip(kinetic, pairs)]

    all_sp = rsp.at[pl.ds(0, 255)]
    arrived(all_sp, bulk_r.at[1])
    planes = rsp.reshape(256, 128)[...] * (1.0 / CELLS)
    crossed = pltpu.roll(planes, 64, 1)
    crossed = jnp.where(low, crossed, -crossed)
    spectrum = product(pair(in_column, 0, 512), split(jnp.concatenate([planes, crossed], axis=0)))
    hartree = (4.0 * np.pi) * (spectrum * spectrum) * inverse
    weighting = 2.0 * hartree * inverse + spectrum * local

    sum_h = down(hartree)
    sum_1, sum_z, sum_zz = down(weighting), down(weighting * fz), down(weighting * fz * fz)
    fy1 = fy[0:1]
    spectral = [
        fx * fx * sum_1 - sum_h, fy1 * fy1 * sum_1 - sum_h, sum_zz - sum_h, fy1 * sum_z, fx * sum_z, fx * fy1 * sum_1
    ]

    arrived(rg.at[pl.ds(0, 127)], bulk_r.at[2])
    rg_flat = rg.reshape(256, 128)
    xc = [jnp.zeros((1, 128), F32)] * 6
    for zz in range(2):
        n = dens[zz]
        grads = (gradx[zz], grady[zz], rg_flat[pl.ds(zz, 128, stride=2), :])
        square = grads[0] * grads[0] + grads[1] * grads[1] + grads[2] * grads[2]
        square_held[zz] = square
        room = 4.0 * n * n + 1.0
        kernel = jnp.exp(jnp.log(n) * (-1.0 / 3.0)) * room / (room + square)
        scaled = [kernel * g for g in grads]
        xc = [t + down(scaled[a] * grads[b]) for t, (a, b) in zip(xc, pairs)]

    store_square = pltpu.make_async_copy(square_held, square_out, osem.at[0])
    store_square.start()
    lines = [spectral[a] - kinetic[a] * (1.0 / NPW) - xc[a] * (1.0 / CELLS) for a in range(6)]
    sums = jnp.sum(jnp.concatenate(lines + [jnp.zeros((2, 128), F32)], axis=0), axis=1, keepdims=True)
    diagonal = lax.broadcasted_iota(jnp.int32, (8, 128), 0) == lax.broadcasted_iota(jnp.int32, (8, 128), 1)
    held[0] = down(jnp.where(diagonal, sums, 0.0))

    plane_me = (x * 4 + y) * 2 + c
    stages = ((tot_z, z, [at(z_=p) for p in z_peers], 8), (tot_p, plane_me, plane, 32))
    for stage, (slots, mine, peers, count) in enumerate(stages):
        for peer in peers:
            pltpu.make_async_remote_copy(
                src_ref=held.at[stage], dst_ref=slots.at[mine], send_sem=ssem.at[1], recv_sem=bulk_r.at[3 + stage],
                device_id=peer, device_id_type=MESH,
            ).start()
        slots[mine] = held[stage]
        if stage == 1:
            arrived(rz, rsem.at[12])
            weight = ab[z]
            for d in range(7):
                weight = weight + rz[d]
            weight = weight.reshape(16, 128)
            g = [wave(a, z) for a in range(3)]
            density[...] = 0.5 * (g[0] * g[0] + g[1] * g[1] + g[2] * g[2]) * weight
            store_density = pltpu.make_async_copy(density, density_out, osem.at[1])
            store_density.start()
        arrived(slots.at[pl.ds(0, count - 1)], bulk_r.at[3 + stage])
        held[stage + 1] = down(slots.reshape(count, 128)[...])
    store_totals = pltpu.make_async_copy(held.at[2], totals_out, osem.at[2])
    store_totals.start()

    arrived(coef.at[:, pl.ds(0, 4544)], ssem.at[0])
    arrived(sp.at[pl.ds(0, 38)], ssem.at[1])
    for k, ref in ((0, all_n), (1, all_sp), (2, all_n)):
        arrived(ref, bulk_s.at[k])
    store_square.wait()
    store_density.wait()
    store_totals.wait()


def emit_kernel(totals_any, density_any, square_any, stress_out, density_out, square_out, totals, stress, density, square, sem):
    into = [
        pltpu.make_async_copy(src, dst, sem.at[k])
        for k, (src, dst) in enumerate(((square_any, square), (density_any, density), (totals_any, totals)))
    ]
    for copy in into:
        copy.start()
    out = [
        pltpu.make_async_copy(src, dst, sem.at[3 + k])
        for k, (src, dst) in enumerate(((square, square_out), (density, density_out), (stress, stress_out)))
    ]
    for k in range(2):
        into[k].wait()
        out[k].start()
    into[2].wait()
    for a in range(6):
        stress[a] = totals[0, a]
    out[2].start()
    for copy in out:
        copy.wait()


def shards(coefficients, occupation, miller, density, local_factor):
    pairs = coefficients[0].reshape(2, 2, NPW // 128, 128).transpose(0, 2, 1, 3).reshape(2, NPW // 64, 128)
    in_plane, in_column = [jnp.asarray(t) for t in tables()]
    hbm = pl.BlockSpec(memory_space=pltpu.HBM)
    millers = miller.reshape(3, 16, 128).transpose(1, 0, 2)
    loaded = [((8, 16, 3, 128), jnp.int32), (pairs.shape, BF16), ((2, 128, 128), F32), ((128, 128), F32), ((2, 256, 128), F32)]
    loaded += [(t.shape, BF16) for t in (in_plane, in_column)]
    scratch = loaded + [
        (shape, F32)
        for shape in (
            (128, 2, 128), (128, 2, 128), (128, 2, 128), (128, 2, 128), (256, 1, 128), (256, 1, 128),
            (64, 2, 32, 128), (64, 32, 128), (4, 32, 8, 128), (4, 32, 8, 128), (2, 32, 8, 128), (2, 32, 8, 128),
            (4, 16, 8, 128), (4, 16, 8, 128),
            (4, 8, 8, 128), (4, 8, 8, 128), (3, 8, 8, 128), (3, 8, 8, 128), (8, 2, 8, 128), (7, 2, 8, 128), (2, 128, 128),
            (3, 1, 128), (8, 1, 128), (32, 1, 128), (16, 128), (2, 128, 128),
            (2, 128, 128), (2, 128, 128),
        )
    ]
    dma = pltpu.SemaphoreType.DMA
    results = (
        jax.ShapeDtypeStruct((1, 128), F32),
        jax.ShapeDtypeStruct((16, 128), F32),
        jax.ShapeDtypeStruct((2, 128, 128), F32),
    )
    totals, kinetic_density, square = pl.pallas_call(
        stress_kernel,
        out_shape=results,
        in_specs=[hbm] * 7,
        out_specs=(hbm,) * 3,
        scratch_shapes=[pltpu.SMEM((1, 2), jnp.int32)]
        + [pltpu.VMEM(*one) for one in scratch]
        + [pltpu.SemaphoreType.REGULAR, dma((10,)), dma((3,)), dma((2,)), dma((13,)), dma((3,)), dma((5,))],
        compiler_params=pltpu.CompilerParams(collective_id=0, has_side_effects=True),
    )(occupation, millers, pairs, density[0], local_factor.reshape(2, 256, 128), in_plane, in_column)
    stress, kinetic_density, square = pl.pallas_call(
        emit_kernel,
        out_shape=(jax.ShapeDtypeStruct((6,), F32),) + results[1:],
        in_specs=[hbm] * 3,
        out_specs=(hbm,) * 3,
        scratch_shapes=[
            pltpu.SMEM((1, 128), F32),
            pltpu.SMEM((6,), F32),
            pltpu.VMEM((16, 128), F32),
            pltpu.VMEM((2, 128, 128), F32),
            dma((6,)),
        ],
    )(totals, kinetic_density, square)
    return (stress, kinetic_density.reshape(-1), square[None])


def solution(mesh):
    return jax.shard_map(
        shards,
        mesh=mesh,
        in_specs=(
            P("spin", None, "band", None),
            P("spin", "band"),
            P(None, ("band", "spin")),
            P("spin", "band", None, None),
            P(None, None, "band", None),
        ),
        out_specs=(P(), P(("band", "spin")), P("spin", "band", None, None)),
        check_vma=False,
    )
```

time: 47.6 us -> 44.6 us (0.937)
  Pallas kernels: 46.9 us -> 43.9 us
    pallas_call x1, Pallas kernels: 45.2 us -> 42.3 us  [shards(): pl.pallas_call(stress_kernel, out_shape=results, in_specs=[hbm] * 7, out_...]
where the time goes in v5:
time: 44.6 us; the launch traced here: 44.5 us
  Pallas kernels  43.9 us (98%)
  between operations  0.64 us (1%)
    pallas_call x1, Pallas kernels, shards(): pl.pallas_call(stress_kernel, out_shape=results, in_specs=[hbm] * 7, out_...  42.3 us
    pallas_call x1, Pallas kernels, shards(): pl.pallas_call(emit_kernel, out_shape=(jax.ShapeDtypeStruct((6,), F32),)...  1.62 us

profile of v5, /device:TPU:1, one launch (start us, length us, event | category | flops | bytes accessed | tf_op | source)
XLA Modules:
  0.0 44.5 jit_solution(11833080912639158610)
XLA Ops:
  0.6 42.3 %shard_map.94 = (f32[1,128]{1,0:T(1,128)}, f32[16,128]{1,0:T(8,128)}, f32[2,128,128]{2,1,0:T(8,128)}) custom-call(s32[1,2]{1,0:T(1,128)} %occ_any.1, s32[16,3,128]{2,1,0:T(4,128)} %bitcast.15, bf16[2,8192,128]{2,1,0:T(8,128)(2,1)} %bitcast.12, f32[2,128,128]{2,1,0:T(8,128)} %bitcast.14, f32[2,256,128]{2,1,0:T(8,128)} %bitcast.13, ...), custom_call_target="tpu_custom_call" | custom-call | tf_op jit(solution)/shard_map/pallas_call | solution.py:429
  42.9 1.6 %shard_map.95 = (f32[6]{0:T(128)}, f32[16,128]{1,0:T(8,128)}, f32[2,128,128]{2,1,0:T(8,128)}) custom-call(f32[1,128]{1,0:T(1,128)} %get-tuple-element.9.totals_any, f32[16,128]{1,0:T(8,128)} %get-tuple-element.10.density_any, f32[2,128,128]{2,1,0:T(8,128)} %get-tuple-element.11.square_any), custom_call_target="tpu_custom_call" | custom-call | tf_op jit(solution)/shard_map/pallas_call | solution.py:439

commit v6 on v5

--- a/solution.py
+++ b/solution.py
@@ -52,7 +52,8 @@
     along_x = np.concatenate([cos_x, sin_x], axis=1)
     along_z = np.concatenate([cos_z, sin_z], axis=1)
     plane = np.concatenate([along_y, along_x, derivative_table(NX)], axis=1)
-    column = np.concatenate([along_z, derivative_table(NZ)], axis=1)
+    order = np.concatenate([np.arange(0, NZ, 2), np.arange(1, NZ, 2)])
+    column = np.concatenate([along_z, derivative_table(NZ)[order][:, order]], axis=1)
     return [halves(t) for t in (plane, column)]
 
 
@@ -79,7 +80,7 @@
     sn, rn, gz, rg, sp, rsp,
     part, twin, qa, qb, ra, rb, ha, hb, a1, b1, ra2, rb2, ab, rz, tmp,
     held, tot_z, tot_p, density, square_held,
-    gradx, grady, far, lsem, osem, ssem, rsem, bulk_s, bulk_r,
+    far, lsem, osem, ssem, rsem, bulk_s, bulk_r,
 ):
     band, s = lax.axis_index("band"), lax.axis_index("spin")
     x_lo, z, y, c = band // 64, lax.rem(band // 8, 8), lax.rem(band // 2, 4), lax.rem(band, 2)
@@ -162,16 +163,12 @@
     for p in z_peers:
         send(millers.at[z], millers.at[z], 5, at(z_=p))
 
-    sn_flat = sn.reshape(256, 128)
-    for zz in range(2):
-        sn_flat[pl.ds(zz, 128, stride=2), :] = dens[zz]
-
     load_plane.wait()
-    from_y = product(split(dens[...].reshape(256, 128)), pair(in_plane, 512, 640))
+    sn_flat = sn.reshape(512, 128)
     from_x = product(pair(in_plane, 896, 1024), split(jnp.concatenate([dens[0], dens[1]], axis=1)))
     for zz in range(2):
-        grady[zz] = from_y[zz * 128 : zz * 128 + 128]
-        gradx[zz] = from_x[:, zz * 128 : zz * 128 + 128]
+        sn_flat[pl.ds(zz, 128, stride=4), :] = dens[zz]
+        sn_flat[pl.ds(2 + zz, 128, stride=4), :] = from_x[:, zz * 128 : zz * 128 + 128]
 
     for q in range(4):
         twins[q].wait_recv()
@@ -258,7 +255,17 @@
     load_column.wait()
     all_n = rn.at[pl.ds(0, 127)]
     arrived(all_n, bulk_r.at[0])
-    gz.reshape(256, 128)[...] = product(pair(in_column, 512, 768), split(rn.reshape(256, 128)[...]))
+    rn_flat = rn.reshape(512, 128)
+    n, grad_x = [
+        jnp.concatenate([rn_flat[pl.ds(k, 128, stride=4), :], rn_flat[pl.ds(k + 1, 128, stride=4), :]], axis=0)
+        for k in (0, 2)
+    ]
+    halves_n = split(n)
+    grads = (grad_x, product(halves_n, pair(in_plane, 512, 640)), product(pair(in_column, 512, 768), halves_n))
+    square = grads[0] * grads[0] + grads[1] * grads[1] + grads[2] * grads[2]
+    gz_flat = gz.reshape(256, 128)
+    for zz in range(2):
+        gz_flat[pl.ds(zz, 128, stride=2), :] = square[zz * 128 : zz * 128 + 128]
 
     def push_back(t, carry):
         pltpu.make_async_remote_copy(
@@ -270,6 +277,15 @@
     lax.fori_loop(band + 1, 128, push_back, 0)
     lax.fori_loop(0, band, push_back, 0)
     rg[band] = gz[band]
+
+    def down(value):
+        return jnp.sum(value, axis=0, keepdims=True)
+
+    pairs = ((0, 0), (1, 1), (2, 2), (1, 2), (0, 2), (0, 1))
+    room = 4.0 * n * n + 1.0
+    kernel = jnp.exp(jnp.log(n) * (-1.0 / 3.0)) * room / (room + square)
+    scaled_grads = [kernel * g for g in grads]
+    xc = [down(scaled_grads[a] * grads[b]) for a, b in pairs]
 
     load_factor.wait()
     lane = lax.broadcasted_iota(jnp.int32, (256, 128), 1)
@@ -295,10 +311,6 @@
     for d, p in enumerate(z_peers):
         send(ab.at[p], rz.at[d], 12, at(z_=p))
 
-    def down(value):
-        return jnp.sum(value, axis=0, keepdims=True)
-
-    pairs = ((0, 0), (1, 1), (2, 2), (1, 2), (0, 2), (0, 1))
     arrived(millers.at[pl.ds(0, 7)], rsem.at[5])
 
     def wave(a, at_z):
@@ -327,21 +339,6 @@
         fx * fx * sum_1 - sum_h, fy1 * fy1 * sum_1 - sum_h, sum_zz - sum_h, fy1 * sum_z, fx * sum_z, fx * fy1 * sum_1
     ]
 
-    arrived(rg.at[pl.ds(0, 127)], bulk_r.at[2])
-    rg_flat = rg.reshape(256, 128)
-    xc = [jnp.zeros((1, 128), F32)] * 6
-    for zz in range(2):
-        n = dens[zz]
-        grads = (gradx[zz], grady[zz], rg_flat[pl.ds(zz, 128, stride=2), :])
-        square = grads[0] * grads[0] + grads[1] * grads[1] + grads[2] * grads[2]
-        square_held[zz] = square
-        room = 4.0 * n * n + 1.0
-        kernel = jnp.exp(jnp.log(n) * (-1.0 / 3.0)) * room / (room + square)
-        scaled = [kernel * g for g in grads]
-        xc = [t + down(scaled[a] * grads[b]) for t, (a, b) in zip(xc, pairs)]
-
-    store_square = pltpu.make_async_copy(square_held, square_out, osem.at[0])
-    store_square.start()
     lines = [spectral[a] - kinetic[a] * (1.0 / NPW) - xc[a] * (1.0 / CELLS) for a in range(6)]
     sums = jnp.sum(jnp.concatenate(lines + [jnp.zeros((2, 128), F32)], axis=0), axis=1, keepdims=True)
     diagonal = lax.broadcasted_iota(jnp.int32, (8, 128), 0) == lax.broadcasted_iota(jnp.int32, (8, 128), 1)
@@ -366,6 +363,12 @@
             density[...] = 0.5 * (g[0] * g[0] + g[1] * g[1] + g[2] * g[2]) * weight
             store_density = pltpu.make_async_copy(density, density_out, osem.at[1])
             store_density.start()
+            arrived(rg.at[pl.ds(0, 127)], bulk_r.at[2])
+            rg_flat = rg.reshape(256, 128)
+            for zz in range(2):
+                square_held[zz] = rg_flat[pl.ds(zz, 128, stride=2), :]
+            store_square = pltpu.make_async_copy(square_held, square_out, osem.at[0])
+            store_square.start()
         arrived(slots.at[pl.ds(0, count - 1)], bulk_r.at[3 + stage])
         held[stage + 1] = down(slots.reshape(count, 128)[...])
     store_totals = pltpu.make_async_copy(held.at[2], totals_out, osem.at[2])
@@ -373,7 +376,7 @@
 
     arrived(coef.at[:, pl.ds(0, 4544)], ssem.at[0])
     arrived(sp.at[pl.ds(0, 38)], ssem.at[1])
-    for k, ref in ((0, all_n), (1, all_sp), (2, all_n)):
+    for k, ref in ((0, all_n), (1, all_sp), (2, rg.at[pl.ds(0, 127)])):
         arrived(ref, bulk_s.at[k])
     store_square.wait()
     store_density.wait()
@@ -412,12 +415,11 @@
     scratch = loaded + [
         (shape, F32)
         for shape in (
-            (128, 2, 128), (128, 2, 128), (128, 2, 128), (128, 2, 128), (256, 1, 128), (256, 1, 128),
+            (128, 4, 128), (128, 4, 128), (128, 2, 128), (128, 2, 128), (256, 1, 128), (256, 1, 128),
             (64, 2, 32, 128), (64, 32, 128), (4, 32, 8, 128), (4, 32, 8, 128), (2, 32, 8, 128), (2, 32, 8, 128),
             (4, 16, 8, 128), (4, 16, 8, 128),
             (4, 8, 8, 128), (4, 8, 8, 128), (3, 8, 8, 128), (3, 8, 8, 128), (8, 2, 8, 128), (7, 2, 8, 128), (2, 128, 128),
             (3, 1, 128), (8, 1, 128), (32, 1, 128), (16, 128), (2, 128, 128),
-            (2, 128, 128), (2, 128, 128),
         )
     ]
     dma = pltpu.SemaphoreType.DMA

time: 44.6 us -> 42 us (0.942)
  Pallas kernels: 43.9 us -> 41.3 us
    pallas_call x1, Pallas kernels: 42.3 us -> 39.7 us  [shards(): pl.pallas_call(stress_kernel, out_shape=results, in_specs=[hbm] * 7, out_...]
where the time goes in v6:
time: 42 us; the launch traced here: 41.9 us
  Pallas kernels  41.3 us (98%)
  between operations  0.64 us (2%)
    pallas_call x1, Pallas kernels, shards(): pl.pallas_call(stress_kernel, out_shape=results, in_specs=[hbm] * 7, out_...  39.7 us
    pallas_call x1, Pallas kernels, shards(): pl.pallas_call(emit_kernel, out_shape=(jax.ShapeDtypeStruct((6,), F32),)...  1.62 us

profile of v6, /device:TPU:1, one launch (start us, length us, event | category | flops | bytes accessed | tf_op | source)
XLA Modules:
  0.0 41.9 jit_solution(3641945143353718467)
XLA Ops:
  0.6 39.7 %shard_map.94 = (f32[1,128]{1,0:T(1,128)}, f32[16,128]{1,0:T(8,128)}, f32[2,128,128]{2,1,0:T(8,128)}) custom-call(s32[1,2]{1,0:T(1,128)} %occ_any.1, s32[16,3,128]{2,1,0:T(4,128)} %bitcast.15, bf16[2,8192,128]{2,1,0:T(8,128)(2,1)} %bitcast.12, f32[2,128,128]{2,1,0:T(8,128)} %bitcast.14, f32[2,256,128]{2,1,0:T(8,128)} %bitcast.13, ...), custom_call_target="tpu_custom_call" | custom-call | tf_op jit(solution)/shard_map/pallas_call | solution.py:431
  40.3 1.6 %shard_map.95 = (f32[6]{0:T(128)}, f32[16,128]{1,0:T(8,128)}, f32[2,128,128]{2,1,0:T(8,128)}) custom-call(f32[1,128]{1,0:T(1,128)} %get-tuple-element.9.totals_any, f32[16,128]{1,0:T(8,128)} %get-tuple-element.10.density_any, f32[2,128,128]{2,1,0:T(8,128)} %get-tuple-element.11.square_any), custom_call_target="tpu_custom_call" | custom-call | tf_op jit(solution)/shard_map/pallas_call | solution.py:441

commit v7 on v6

--- a/solution.py
+++ b/solution.py
@@ -267,17 +267,6 @@
     for zz in range(2):
         gz_flat[pl.ds(zz, 128, stride=2), :] = square[zz * 128 : zz * 128 + 128]
 
-    def push_back(t, carry):
-        pltpu.make_async_remote_copy(
-            src_ref=gz.at[t], dst_ref=rg.at[band], send_sem=bulk_s.at[2], recv_sem=bulk_r.at[2],
-            device_id={"band": t}, device_id_type=MESH,
-        ).start()
-        return carry
-
-    lax.fori_loop(band + 1, 128, push_back, 0)
-    lax.fori_loop(0, band, push_back, 0)
-    rg[band] = gz[band]
-
     def down(value):
         return jnp.sum(value, axis=0, keepdims=True)
 
@@ -344,6 +333,13 @@
     diagonal = lax.broadcasted_iota(jnp.int32, (8, 128), 0) == lax.broadcasted_iota(jnp.int32, (8, 128), 1)
     held[0] = down(jnp.where(diagonal, sums, 0.0))
 
+    def push_back(t, carry):
+        pltpu.make_async_remote_copy(
+            src_ref=gz.at[t], dst_ref=rg.at[band], send_sem=bulk_s.at[2], recv_sem=bulk_r.at[2],
+            device_id={"band": t}, device_id_type=MESH,
+        ).start()
+        return carry
+
     plane_me = (x * 4 + y) * 2 + c
     stages = ((tot_z, z, [at(z_=p) for p in z_peers], 8), (tot_p, plane_me, plane, 32))
     for stage, (slots, mine, peers, count) in enumerate(stages):
@@ -353,6 +349,10 @@
                 device_id=peer, device_id_type=MESH,
             ).start()
         slots[mine] = held[stage]
+        if stage == 0:
+            lax.fori_loop(band + 1, 128, push_back, 0)
+            lax.fori_loop(0, band, push_back, 0)
+            rg[band] = gz[band]
         if stage == 1:
             arrived(rz, rsem.at[12])
             weight = ab[z]
@@ -363,16 +363,16 @@
             density[...] = 0.5 * (g[0] * g[0] + g[1] * g[1] + g[2] * g[2]) * weight
             store_density = pltpu.make_async_copy(density, density_out, osem.at[1])
             store_density.start()
-            arrived(rg.at[pl.ds(0, 127)], bulk_r.at[2])
-            rg_flat = rg.reshape(256, 128)
-            for zz in range(2):
-                square_held[zz] = rg_flat[pl.ds(zz, 128, stride=2), :]
-            store_square = pltpu.make_async_copy(square_held, square_out, osem.at[0])
-            store_square.start()
         arrived(slots.at[pl.ds(0, count - 1)], bulk_r.at[3 + stage])
         held[stage + 1] = down(slots.reshape(count, 128)[...])
     store_totals = pltpu.make_async_copy(held.at[2], totals_out, osem.at[2])
     store_totals.start()
+    arrived(rg.at[pl.ds(0, 127)], bulk_r.at[2])
+    rg_flat = rg.reshape(256, 128)
+    for zz in range(2):
+        square_held[zz] = rg_flat[pl.ds(zz, 128, stride=2), :]
+    store_square = pltpu.make_async_copy(square_held, square_out, osem.at[0])
+    store_square.start()
 
     arrived(coef.at[:, pl.ds(0, 4544)], ssem.at[0])
     arrived(sp.at[pl.ds(0, 38)], ssem.at[1])

time: 42 us -> 41.3 us (0.983)
  Pallas kernels: 41.3 us -> 40.6 us
    pallas_call x1, Pallas kernels: 39.7 us -> 39 us  [shards(): pl.pallas_call(stress_kernel, out_shape=results, in_specs=[hbm] * 7, out_...]
where the time goes in v7:
time: 41.3 us; the launch traced here: 41.2 us
  Pallas kernels  40.6 us (98%)
  between operations  0.64 us (2%)
    pallas_call x1, Pallas kernels, shards(): pl.pallas_call(stress_kernel, out_shape=results, in_specs=[hbm] * 7, out_...  39 us
    pallas_call x1, Pallas kernels, shards(): pl.pallas_call(emit_kernel, out_shape=(jax.ShapeDtypeStruct((6,), F32),)...  1.62 us

profile of v7, /device:TPU:1, one launch (start us, length us, event | category | flops | bytes accessed | tf_op | source)
XLA Modules:
  0.0 41.2 jit_solution(5831934464996442163)
XLA Ops:
  0.6 39.0 %shard_map.94 = (f32[1,128]{1,0:T(1,128)}, f32[16,128]{1,0:T(8,128)}, f32[2,128,128]{2,1,0:T(8,128)}) custom-call(s32[1,2]{1,0:T(1,128)} %occ_any.1, s32[16,3,128]{2,1,0:T(4,128)} %bitcast.15, bf16[2,8192,128]{2,1,0:T(8,128)(2,1)} %bitcast.12, f32[2,128,128]{2,1,0:T(8,128)} %bitcast.14, f32[2,256,128]{2,1,0:T(8,128)} %bitcast.13, ...), custom_call_target="tpu_custom_call" | custom-call | tf_op jit(solution)/shard_map/pallas_call | solution.py:431
  39.6 1.6 %shard_map.95 = (f32[6]{0:T(128)}, f32[16,128]{1,0:T(8,128)}, f32[2,128,128]{2,1,0:T(8,128)}) custom-call(f32[1,128]{1,0:T(1,128)} %get-tuple-element.9.totals_any, f32[16,128]{1,0:T(8,128)} %get-tuple-element.10.density_any, f32[2,128,128]{2,1,0:T(8,128)} %get-tuple-element.11.square_any), custom_call_target="tpu_custom_call" | custom-call | tf_op jit(solution)/shard_map/pallas_call | solution.py:441

commit v8 on v7

--- a/solution.py
+++ b/solution.py
@@ -159,9 +159,6 @@
     over_spin = send(dens.at[1 - s], far_plane, 4, at(x_=x_peers[1]))
     for p in z_peers:
         pl.semaphore_signal(far, inc=1, device_id=at(z_=p), device_id_type=MESH)
-    load_miller.wait()
-    for p in z_peers:
-        send(millers.at[z], millers.at[z], 5, at(z_=p))
 
     load_plane.wait()
     sn_flat = sn.reshape(512, 128)
@@ -205,6 +202,10 @@
     lax.fori_loop(band + 1, 128, push_density, 0)
     lax.fori_loop(0, band, push_density, 0)
     rn[band] = sn[band]
+
+    load_miller.wait()
+    for p in z_peers:
+        send(millers.at[z], millers.at[z], 5, at(z_=p))
 
     for own, got, half, (right, across, left), where, k in rings:
         send(own.at[right, low_half], got.at[0, low_half], k + 1, where(right))

time: 41.3 us -> 44.9 us (1.087)
  Pallas kernels: 40.6 us -> 44.2 us
    pallas_call x1, Pallas kernels: 39 us -> 42.5 us  [shards(): pl.pallas_call(stress_kernel, out_shape=results, in_specs=[hbm] * 7, out_...]
where the time goes in v8:
time: 44.9 us; the launch traced here: 44.8 us
  Pallas kernels  44.2 us (98%)
  between operations  0.64 us (1%)
    pallas_call x1, Pallas kernels, shards(): pl.pallas_call(stress_kernel, out_shape=results, in_specs=[hbm] * 7, out_...  42.5 us
    pallas_call x1, Pallas kernels, shards(): pl.pallas_call(emit_kernel, out_shape=(jax.ShapeDtypeStruct((6,), F32),)...  1.62 us

profile of v8, /device:TPU:1, one launch (start us, length us, event | category | flops | bytes accessed | tf_op | source)
XLA Modules:
  0.0 44.8 jit_solution(7164034371150124131)
XLA Ops:
  0.6 42.5 %shard_map.94 = (f32[1,128]{1,0:T(1,128)}, f32[16,128]{1,0:T(8,128)}, f32[2,128,128]{2,1,0:T(8,128)}) custom-call(s32[1,2]{1,0:T(1,128)} %occ_any.1, s32[16,3,128]{2,1,0:T(4,128)} %bitcast.15, bf16[2,8192,128]{2,1,0:T(8,128)(2,1)} %bitcast.12, f32[2,128,128]{2,1,0:T(8,128)} %bitcast.14, f32[2,256,128]{2,1,0:T(8,128)} %bitcast.13, ...), custom_call_target="tpu_custom_call" | custom-call | tf_op jit(solution)/shard_map/pallas_call | solution.py:432
  43.2 1.6 %shard_map.95 = (f32[6]{0:T(128)}, f32[16,128]{1,0:T(8,128)}, f32[2,128,128]{2,1,0:T(8,128)}) custom-call(f32[1,128]{1,0:T(1,128)} %get-tuple-element.9.totals_any, f32[16,128]{1,0:T(8,128)} %get-tuple-element.10.density_any, f32[2,128,128]{2,1,0:T(8,128)} %get-tuple-element.11.square_any), custom_call_target="tpu_custom_call" | custom-call | tf_op jit(solution)/shard_map/pallas_call | solution.py:442
